TPU v7x, 8 devices: a whole 2x2x1 slice. The times are simulated.
8 devices in a mesh: dp: 1 (over z), cpo: 2 (over y), cp: 4 (over x, core).
Axes of the slice: x: 2, y: 2, z: 1, core: 2. Of those that a mesh axis runs over, the one named last changes fastest.
Arguments:
- queries: bfloat16 [4096, 3, 128], P(('dp', 'cpo', 'cp'))
- keys: bfloat16 [4096, 128], P(('dp', 'cpo', 'cp'))
- values: bfloat16 [4096, 128], P(('dp', 'cpo', 'cp'))
- attn_out: bfloat16 [4096, 3, 128], P(('dp', 'cpo', 'cp'))
- logsumexp: float32 [4096, 3], P(('dp', 'cpo', 'cp'))
- d_out: bfloat16 [4096, 3, 128], P(('dp', 'cpo', 'cp'))
- cu_seqlens: int32 [14], P('dp')
Outputs:
- output 1: bfloat16 [4096, 3, 128], P(('dp', 'cpo', 'cp'))
- output 2: bfloat16 [4096, 128], P(('dp', 'cpo', 'cp'))
- output 3: bfloat16 [4096, 128], P(('dp', 'cpo', 'cp'))
All inputs are finite; a program needn't handle non-finite values.
Results may differ from a plain program's by a relative error of at most 0.001.
Values are sent between devices in bfloat16 or wider.
A program may use at most 1 GiB of HBM per device.

v0:
```python
import jax
import jax.numpy as jnp
from jax import lax
from jax.sharding import PartitionSpec as P

HOPS = 3


def doc_ids(bounds, positions, seq_len):
    found = jnp.searchsorted(bounds[1:], positions, side="right").astype(jnp.int32)
    return jnp.where((positions >= 0) & (positions < seq_len), found, -1)


def window_backward(q_loc, do_loc, lse_loc, dot_loc, id_q, pos_q, k_win, v_win, id_k, pos_k, scale):
    rows, heads, head = q_loc.shape
    block_rows = min(64, rows)
    count = rows // block_rows
    blocks = (
        q_loc.reshape(count, block_rows, heads, head),
        do_loc.reshape(count, block_rows, heads, head),
        lse_loc.reshape(count, block_rows, heads),
        dot_loc.reshape(count, block_rows, heads),
        id_q.reshape(count, block_rows),
        pos_q.reshape(count, block_rows),
    )

    def step(carry, block):
        dk_acc, dv_acc = carry
        q_blk, do_blk, lse_blk, dot_blk, idq_blk, posq_blk = block
        keep = (idq_blk[:, None] == id_k[None, :]) & (pos_k[None, :] <= posq_blk[:, None])
        scores = jnp.einsum("qgd,kd->qgk", q_blk, k_win, preferred_element_type=jnp.float32)
        p_mat = jnp.where(keep[:, None, :], jnp.exp(scale * scores - lse_blk[:, :, None]), 0.0)
        dp_mat = jnp.einsum("qgd,kd->qgk", do_blk, v_win, preferred_element_type=jnp.float32)
        ds_mat = (p_mat * (dp_mat - dot_blk[:, :, None])).astype(jnp.bfloat16)
        dq_blk = scale * jnp.einsum("qgk,kd->qgd", ds_mat, k_win, preferred_element_type=jnp.float32)
        dk_acc = dk_acc + jnp.einsum("qgk,qgd->kd", ds_mat, q_blk, preferred_element_type=jnp.float32)
        dv_acc = dv_acc + jnp.einsum("qgk,qgd->kd", p_mat.astype(jnp.bfloat16), do_blk, preferred_element_type=jnp.float32)
        return (dk_acc, dv_acc), dq_blk.astype(jnp.bfloat16)

    width = k_win.shape[0]
    init = (jnp.zeros((width, head), jnp.float32), jnp.zeros((width, head), jnp.float32))
    (dk_sum, dv_sum), dq_blocks = lax.scan(step, init, blocks)
    return dq_blocks.reshape(rows, heads, head), dk_sum, dv_sum


def solution(mesh):
    inner = mesh.shape["cp"]
    group = mesh.shape["cpo"] * inner
    seq_axes = ("cpo", "cp")

    def local(queries, keys, values, attn_out, logsumexp, d_out, cu_seqlens):
        rows, heads, head = queries.shape
        scale = head ** -0.5
        seq_len = group * rows
        rank = lax.axis_index("cpo") * inner + lax.axis_index("cp")
        kv_pair = jnp.stack([keys, values])
        received = []
        for hop in range(HOPS, 0, -1):
            received.append(lax.ppermute(kv_pair, seq_axes, [(sender, sender + hop) for sender in range(group - hop)]))
        received.append(kv_pair)
        kv_win = jnp.concatenate(received, axis=1)
        pos_q = rank * rows + jnp.arange(rows, dtype=jnp.int32)
        pos_k = (rank - HOPS) * rows + jnp.arange((HOPS + 1) * rows, dtype=jnp.int32)
        id_q = doc_ids(cu_seqlens, pos_q, seq_len)
        id_k = doc_ids(cu_seqlens, pos_k, seq_len)
        row_dot = jnp.einsum("qgd,qgd->qg", d_out, attn_out, preferred_element_type=jnp.float32)
        d_query, dk_sum, dv_sum = window_backward(queries, d_out, logsumexp, row_dot, id_q, pos_q, kv_win[0], kv_win[1], id_k, pos_k, scale)
        part_sums = jnp.stack([dk_sum, dv_sum]).reshape(2, HOPS + 1, rows, head)
        owned = part_sums[:, HOPS]
        for hop in range(1, HOPS + 1):
            owned = owned + lax.ppermute(part_sums[:, HOPS - hop], seq_axes, [(sender, sender - hop) for sender in range(hop, group)])
        return d_query, (scale * owned[0]).astype(jnp.bfloat16), owned[1].astype(jnp.bfloat16)

    seq_spec = P(("dp", "cpo", "cp"))
    return jax.shard_map(local, mesh=mesh, in_specs=(seq_spec, seq_spec, seq_spec, seq_spec, seq_spec, seq_spec, P("dp")), out_specs=(seq_spec, seq_spec, seq_spec), check_vma=False)
```

profile of v0, /device:TPU:3, one launch (start us, length us, event | category | flops | bytes accessed | tf_op | source)
XLA Modules:
  0.0 197.4 jit_solution(9171975629193432184)
XLA Ops:
  1.7 3.7 %collective-permute-start = (bf16[2,512,128]{2,1,0:T(8,128)(2,1)S(1)}, bf16[2,512,128]{2,1,0:T(8,128)(2,1)S(1)}, u32[]{:S(2)}, u32[]{:S(2)}) collective-permute-start(bf16[2,512,128]{2,1,0:T(8,128)(2,1)S(1)} %pad_maximum_fusion.1), channel_id=1, source_target_pairs={{0,3},{1,4},{2,5},{3,6},{4,7}} | collective-permute-start | bytes 786440 | tf_op jit(solution)/shard_map/ppermute | solution.py:59
  7.4 2.8 %collective-permute-start.2 = (bf16[2,512,128]{2,1,0:T(8,128)(2,1)S(1)}, bf16[2,512,128]{2,1,0:T(8,128)(2,1)S(1)}, u32[]{:S(2)}, u32[]{:S(2)}) collective-permute-start(bf16[2,512,128]{2,1,0:T(8,128)(2,1)S(1)} %pad_maximum_fusion.1), channel_id=1, source_target_pairs={{0,1},{1,2},{2,3},{3,4},{4,5},{5,6},{6,7}} | collective-permute-start | bytes 786440 | tf_op jit(solution)/shard_map/ppermute | solution.py:59
  11.0 35.9 %while.64 = (s32[]{:T(128)}, u32[2048]{0:T(1024)S(1)}, u32[2048]{0:T(1024)S(1)}, s32[13]{0:T(128)S(1)}, s32[]{:T(128)}, /*index=5*/s32[]{:T(128)}, s32[]{:T(128)}) while((s32[]{:T(128)}, u32[2048]{0:T(1024)S(1)}, u32[2048]{0:T(1024)S(1)}, s32[13]{0:T(128)S(1)}, s32[]{:T(128)}, /*index=5*/s32[]{:T(128)}, s32[]{:T(128)}) %tuple.123), condition=%wide.region_3.4_spmd.clone, body=%wide.region_2.3_spmd.clone.sunk | while | flops 67587 | bytes 33015 | solution.py:10
  11.7 8.3 %fusion.85 = (u32[2048]{0:T(1024)S(1)}, u32[2048]{0:T(1024)S(1)}) fusion(u32[2048]{0:T(1024)S(1)} %get-tuple-element.648, u32[2048]{0:T(1024)S(1)} %get-tuple-element.647, s32[]{:T(128)} %get-tuple-element.657, s32[]{:T(128)} %bitcast.161, s32[]{:T(128)} %bitcast.162, s32[]{:T(128)} %bitcast.163, s32[]{:T(128)} %bitcast.164, s32[]{:T(128)} %bitcast.165, ...), kind=kLoop, calls=%fused_computation.8.clone.1 | loop fusion | flops 67584 | bytes 32825 | tf_op jit(solution)/shard_map/jit(searchsorted)/jit(_searchsorted_scan_impl)/vmap(jit(_searchsorted_scan_impl))/while/body/eval_jaxpr/select_n | solution.py:10
  20.7 8.3 %fusion.85 = (u32[2048]{0:T(1024)S(1)}, u32[2048]{0:T(1024)S(1)}) fusion(u32[2048]{0:T(1024)S(1)} %get-tuple-element.648, u32[2048]{0:T(1024)S(1)} %get-tuple-element.647, s32[]{:T(128)} %get-tuple-element.657, s32[]{:T(128)} %bitcast.161, s32[]{:T(128)} %bitcast.162, s32[]{:T(128)} %bitcast.163, s32[]{:T(128)} %bitcast.164, s32[]{:T(128)} %bitcast.165, ...), kind=kLoop, calls=%fused_computation.8.clone.1 | loop fusion | flops 67584 | bytes 32825 | tf_op jit(solution)/shard_map/jit(searchsorted)/jit(_searchsorted_scan_impl)/vmap(jit(_searchsorted_scan_impl))/while/body/eval_jaxpr/select_n | solution.py:10
  29.7 8.3 %fusion.85 = (u32[2048]{0:T(1024)S(1)}, u32[2048]{0:T(1024)S(1)}) fusion(u32[2048]{0:T(1024)S(1)} %get-tuple-element.648, u32[2048]{0:T(1024)S(1)} %get-tuple-element.647, s32[]{:T(128)} %get-tuple-element.657, s32[]{:T(128)} %bitcast.161, s32[]{:T(128)} %bitcast.162, s32[]{:T(128)} %bitcast.163, s32[]{:T(128)} %bitcast.164, s32[]{:T(128)} %bitcast.165, ...), kind=kLoop, calls=%fused_computation.8.clone.1 | loop fusion | flops 67584 | bytes 32825 | tf_op jit(solution)/shard_map/jit(searchsorted)/jit(_searchsorted_scan_impl)/vmap(jit(_searchsorted_scan_impl))/while/body/eval_jaxpr/select_n | solution.py:10
  38.7 8.3 %fusion.85 = (u32[2048]{0:T(1024)S(1)}, u32[2048]{0:T(1024)S(1)}) fusion(u32[2048]{0:T(1024)S(1)} %get-tuple-element.648, u32[2048]{0:T(1024)S(1)} %get-tuple-element.647, s32[]{:T(128)} %get-tuple-element.657, s32[]{:T(128)} %bitcast.161, s32[]{:T(128)} %bitcast.162, s32[]{:T(128)} %bitcast.163, s32[]{:T(128)} %bitcast.164, s32[]{:T(128)} %bitcast.165, ...), kind=kLoop, calls=%fused_computation.8.clone.1 | loop fusion | flops 67584 | bytes 32825 | tf_op jit(solution)/shard_map/jit(searchsorted)/jit(_searchsorted_scan_impl)/vmap(jit(_searchsorted_scan_impl))/while/body/eval_jaxpr/select_n | solution.py:10
  46.9 36.0 %while.63 = (s32[]{:T(128)}, u32[512]{0:T(512)S(1)}, u32[512]{0:T(512)S(1)}, s32[13]{0:T(128)S(1)}, s32[]{:T(128)}, /*index=5*/s32[]{:T(128)}, s32[]{:T(128)}) while((s32[]{:T(128)}, u32[512]{0:T(512)S(1)}, u32[512]{0:T(512)S(1)}, s32[13]{0:T(128)S(1)}, s32[]{:T(128)}, /*index=5*/s32[]{:T(128)}, s32[]{:T(128)}) %tuple.129), condition=%wide.region_1.2_spmd.clone, body=%wide.region_0.1_spmd.clone.sunk | while | flops 16899 | bytes 8439 | solution.py:10
  47.7 8.3 %fusion.83 = (u32[512]{0:T(512)S(1)}, u32[512]{0:T(512)S(1)}) fusion(u32[512]{0:T(512)S(1)} %get-tuple-element.627, u32[512]{0:T(512)S(1)} %get-tuple-element.626, s32[]{:T(128)} %get-tuple-element.636, s32[]{:T(128)} %bitcast.148, s32[]{:T(128)} %bitcast.149, s32[]{:T(128)} %bitcast.150, s32[]{:T(128)} %bitcast.151, s32[]{:T(128)} %bitcast.152, ...), kind=kLoop, calls=%fused_computation.5.clone.1 | loop fusion | flops 16896 | bytes 8249 | tf_op jit(solution)/shard_map/jit(searchsorted)/jit(_searchsorted_scan_impl)/vmap(jit(_searchsorted_scan_impl))/while/body/eval_jaxpr/select_n | solution.py:10
  56.7 8.3 %fusion.83 = (u32[512]{0:T(512)S(1)}, u32[512]{0:T(512)S(1)}) fusion(u32[512]{0:T(512)S(1)} %get-tuple-element.627, u32[512]{0:T(512)S(1)} %get-tuple-element.626, s32[]{:T(128)} %get-tuple-element.636, s32[]{:T(128)} %bitcast.148, s32[]{:T(128)} %bitcast.149, s32[]{:T(128)} %bitcast.150, s32[]{:T(128)} %bitcast.151, s32[]{:T(128)} %bitcast.152, ...), kind=kLoop, calls=%fused_computation.5.clone.1 | loop fusion | flops 16896 | bytes 8249 | tf_op jit(solution)/shard_map/jit(searchsorted)/jit(_searchsorted_scan_impl)/vmap(jit(_searchsorted_scan_impl))/while/body/eval_jaxpr/select_n | solution.py:10
  65.7 8.3 %fusion.83 = (u32[512]{0:T(512)S(1)}, u32[512]{0:T(512)S(1)}) fusion(u32[512]{0:T(512)S(1)} %get-tuple-element.627, u32[512]{0:T(512)S(1)} %get-tuple-element.626, s32[]{:T(128)} %get-tuple-element.636, s32[]{:T(128)} %bitcast.148, s32[]{:T(128)} %bitcast.149, s32[]{:T(128)} %bitcast.150, s32[]{:T(128)} %bitcast.151, s32[]{:T(128)} %bitcast.152, ...), kind=kLoop, calls=%fused_computation.5.clone.1 | loop fusion | flops 16896 | bytes 8249 | tf_op jit(solution)/shard_map/jit(searchsorted)/jit(_searchsorted_scan_impl)/vmap(jit(_searchsorted_scan_impl))/while/body/eval_jaxpr/select_n | solution.py:10
  74.7 8.3 %fusion.83 = (u32[512]{0:T(512)S(1)}, u32[512]{0:T(512)S(1)}) fusion(u32[512]{0:T(512)S(1)} %get-tuple-element.627, u32[512]{0:T(512)S(1)} %get-tuple-element.626, s32[]{:T(128)} %get-tuple-element.636, s32[]{:T(128)} %bitcast.148, s32[]{:T(128)} %bitcast.149, s32[]{:T(128)} %bitcast.150, s32[]{:T(128)} %bitcast.151, s32[]{:T(128)} %bitcast.152, ...), kind=kLoop, calls=%fused_computation.5.clone.1 | loop fusion | flops 16896 | bytes 8249 | tf_op jit(solution)/shard_map/jit(searchsorted)/jit(_searchsorted_scan_impl)/vmap(jit(_searchsorted_scan_impl))/while/body/eval_jaxpr/select_n | solution.py:10
  85.5 74.4 %while.65 = (s32[]{:T(128)}, f32[2048,128]{1,0:T(8,128)S(1)}, f32[2048,128]{1,0:T(8,128)}, bf16[8,64,3,128]{3,1,0,2:T(8,128)(2,1)}, s32[8,64]{1,0:T(8,128)S(1)},...) while((s32[]{:T(128)}, f32[2048,128]{1,0:T(8,128)S(1)}, ...), condition=%wide.region_5.6_spmd.clone, body=%wide.region_4.5_spmd.clone.sunk | while | flops 507561984 | bytes 19681024 | solution.py:42
  101.0 2.8 %fusion.100 = f32[2048,128]{1,0:T(8,128)} fusion(f32[2048,128]{1,0:T(8,128)} %get-tuple-element.678, f32[64,3,2048]{2,0,1:T(8,128)S(1)} %fusion.97, pred[]{:T(512)S(6)} %compare.160, bf16[8,64,3,128]{3,1,0,2:T(8,128)(2,1)} %get-tuple-element.702, s32[]{:T(128)} %get-tuple-element.676), kind=kOutput, calls=%fused_computation.22.clone.1 | convolution fusion | flops 101580800 | bytes 3719681 | tf_op jit(solution)/shard_map/while/body/eval_jaxpr/qgk,qgd->kd/dot_general | solution.py:37
  110.4 2.8 %fusion.100 = f32[2048,128]{1,0:T(8,128)} fusion(f32[2048,128]{1,0:T(8,128)} %get-tuple-element.678, f32[64,3,2048]{2,0,1:T(8,128)S(1)} %fusion.97, pred[]{:T(512)S(6)} %compare.160, bf16[8,64,3,128]{3,1,0,2:T(8,128)(2,1)} %get-tuple-element.702, s32[]{:T(128)} %get-tuple-element.676), kind=kOutput, calls=%fused_computation.22.clone.1 | convolution fusion | flops 101580800 | bytes 3719681 | tf_op jit(solution)/shard_map/while/body/eval_jaxpr/qgk,qgd->kd/dot_general | solution.py:37
  119.7 2.8 %fusion.100 = f32[2048,128]{1,0:T(8,128)} fusion(f32[2048,128]{1,0:T(8,128)} %get-tuple-element.678, f32[64,3,2048]{2,0,1:T(8,128)S(1)} %fusion.97, pred[]{:T(512)S(6)} %compare.160, bf16[8,64,3,128]{3,1,0,2:T(8,128)(2,1)} %get-tuple-element.702, s32[]{:T(128)} %get-tuple-element.676), kind=kOutput, calls=%fused_computation.22.clone.1 | convolution fusion | flops 101580800 | bytes 3719681 | tf_op jit(solution)/shard_map/while/body/eval_jaxpr/qgk,qgd->kd/dot_general | solution.py:37
  129.1 2.8 %fusion.100 = f32[2048,128]{1,0:T(8,128)} fusion(f32[2048,128]{1,0:T(8,128)} %get-tuple-element.678, f32[64,3,2048]{2,0,1:T(8,128)S(1)} %fusion.97, pred[]{:T(512)S(6)} %compare.160, bf16[8,64,3,128]{3,1,0,2:T(8,128)(2,1)} %get-tuple-element.702, s32[]{:T(128)} %get-tuple-element.676), kind=kOutput, calls=%fused_computation.22.clone.1 | convolution fusion | flops 101580800 | bytes 3719681 | tf_op jit(solution)/shard_map/while/body/eval_jaxpr/qgk,qgd->kd/dot_general | solution.py:37
  138.4 2.8 %fusion.100 = f32[2048,128]{1,0:T(8,128)} fusion(f32[2048,128]{1,0:T(8,128)} %get-tuple-element.678, f32[64,3,2048]{2,0,1:T(8,128)S(1)} %fusion.97, pred[]{:T(512)S(6)} %compare.160, bf16[8,64,3,128]{3,1,0,2:T(8,128)(2,1)} %get-tuple-element.702, s32[]{:T(128)} %get-tuple-element.676), kind=kOutput, calls=%fused_computation.22.clone.1 | convolution fusion | flops 101580800 | bytes 3719681 | tf_op jit(solution)/shard_map/while/body/eval_jaxpr/qgk,qgd->kd/dot_general | solution.py:37
  147.8 2.8 %fusion.100 = f32[2048,128]{1,0:T(8,128)} fusion(f32[2048,128]{1,0:T(8,128)} %get-tuple-element.678, f32[64,3,2048]{2,0,1:T(8,128)S(1)} %fusion.97, pred[]{:T(512)S(6)} %compare.160, bf16[8,64,3,128]{3,1,0,2:T(8,128)(2,1)} %get-tuple-element.702, s32[]{:T(128)} %get-tuple-element.676), kind=kOutput, calls=%fused_computation.22.clone.1 | convolution fusion | flops 101580800 | bytes 3719681 | tf_op jit(solution)/shard_map/while/body/eval_jaxpr/qgk,qgd->kd/dot_general | solution.py:37
  157.1 2.8 %fusion.100 = f32[2048,128]{1,0:T(8,128)} fusion(f32[2048,128]{1,0:T(8,128)} %get-tuple-element.678, f32[64,3,2048]{2,0,1:T(8,128)S(1)} %fusion.97, pred[]{:T(512)S(6)} %compare.160, bf16[8,64,3,128]{3,1,0,2:T(8,128)(2,1)} %get-tuple-element.702, s32[]{:T(128)} %get-tuple-element.676), kind=kOutput, calls=%fused_computation.22.clone.1 | convolution fusion | flops 101580800 | bytes 3719681 | tf_op jit(solution)/shard_map/while/body/eval_jaxpr/qgk,qgd->kd/dot_general | solution.py:37
  163.5 3.3 %collective-permute-start.4 = (f32[2,512,128]{2,1,0:T(8,128)S(1)}, f32[2,512,128]{2,1,0:T(8,128)S(1)}, u32[]{:S(2)}, u32[]{:S(2)}) collective-permute-start(f32[2,512,128]{2,1,0:T(8,128)S(1)} %get-tuple-element.400), channel_id=1, source_target_pairs={{2,0},{3,1},{4,2},{5,3},{6,4},{7,5}} | collective-permute-start | bytes 1572872 | tf_op jit(solution)/shard_map/ppermute | solution.py:71
  168.7 7.8 %collective-permute-done.3 = f32[2,512,128]{2,1,0:T(8,128)S(1)} collective-permute-done((f32[2,512,128]{2,1,0:T(8,128)S(1)}, f32[2,512,128]{2,1,0:T(8,128)S(1)}, u32[]{:S(2)}, u32[]{:S(2)}) %collective-permute-start.3) | collective-permute-done | bytes 524320 | tf_op jit(solution)/shard_map/ppermute | solution.py:71
  176.4 3.8 %collective-permute-done.4 = f32[2,512,128]{2,1,0:T(8,128)S(1)} collective-permute-done((f32[2,512,128]{2,1,0:T(8,128)S(1)}, f32[2,512,128]{2,1,0:T(8,128)S(1)}, u32[]{:S(2)}, u32[]{:S(2)}) %collective-permute-start.4) | collective-permute-done | bytes 524320 | tf_op jit(solution)/shard_map/ppermute | solution.py:71
  180.2 14.8 %collective-permute-done.5 = f32[2,512,128]{2,1,0:T(8,128)S(1)} collective-permute-done((f32[2,512,128]{2,1,0:T(8,128)S(1)}, f32[2,512,128]{2,1,0:T(8,128)S(1)}, u32[]{:S(2)}, u32[]{:S(2)}) %collective-permute-start.5) | collective-permute-done | bytes 524320 | tf_op jit(solution)/shard_map/ppermute | solution.py:71
  (173 shorter events, 73.8 us)
Async XLA Ops:
  0.6 83.9 %copy-start.4 = (bf16[512,128]{1,0:T(8,128)(2,1)S(1)}, bf16[512,128]{1,0:T(8,128)(2,1)}, u32[]{:S(2)}) copy-start(bf16[512,128]{1,0:T(8,128)(2,1)} %param.14) | copy-start | bytes 393220
  0.6 83.9 %copy-start.3 = (bf16[512,128]{1,0:T(8,128)(2,1)S(1)}, bf16[512,128]{1,0:T(8,128)(2,1)}, u32[]{:S(2)}) copy-start(bf16[512,128]{1,0:T(8,128)(2,1)} %param.15) | copy-start | bytes 393220
  0.7 82.3 %copy-start.5 = (bf16[512,3,128]{2,0,1:T(8,128)(2,1)S(1)}, bf16[512,3,128]{2,0,1:T(8,128)(2,1)}, u32[]{:S(2)}) copy-start(bf16[512,3,128]{2,0,1:T(8,128)(2,1)} %param.16) | copy-start | bytes 1179652
  0.7 83.8 %copy-start.6 = (f32[512,3]{0,1:T(4,128)S(1)}, f32[512,3]{0,1:T(4,128)}, u32[]{:S(2)}) copy-start(f32[512,3]{0,1:T(4,128)} %param.17) | copy-start | bytes 18436
  1.7 82.8 %collective-permute-start = (bf16[2,512,128]{2,1,0:T(8,128)(2,1)S(1)}, bf16[2,512,128]{2,1,0:T(8,128)(2,1)S(1)}, u32[]{:S(2)}, u32[]{:S(2)}) collective-permute-start(bf16[2,512,128]{2,1,0:T(8,128)(2,1)S(1)} %pad_maximum_fusion.1), channel_id=1, source_target_pairs={{0,3},{1,4},{2,5},{3,6},{4,7}} | collective-permute-start | bytes 786440 | tf_op jit(solution)/shard_map/ppermute | solution.py:59
  5.4 79.1 %collective-permute-start.1 = (bf16[2,512,128]{2,1,0:T(8,128)(2,1)S(1)}, bf16[2,512,128]{2,1,0:T(8,128)(2,1)S(1)}, u32[]{:S(2)}, u32[]{:S(2)}) collective-permute-start(bf16[2,512,128]{2,1,0:T(8,128)(2,1)S(1)} %pad_maximum_fusion.1), channel_id=1, source_target_pairs={{0,2},{1,3},{2,4},{3,5},{4,6},{5,7}} | collective-permute-start | bytes 786440 | tf_op jit(solution)/shard_map/ppermute | solution.py:59
  7.4 77.2 %collective-permute-start.2 = (bf16[2,512,128]{2,1,0:T(8,128)(2,1)S(1)}, bf16[2,512,128]{2,1,0:T(8,128)(2,1)S(1)}, u32[]{:S(2)}, u32[]{:S(2)}) collective-permute-start(bf16[2,512,128]{2,1,0:T(8,128)(2,1)S(1)} %pad_maximum_fusion.1), channel_id=1, source_target_pairs={{0,1},{1,2},{2,3},{3,4},{4,5},{5,6},{6,7}} | collective-permute-start | bytes 786440 | tf_op jit(solution)/shard_map/ppermute | solution.py:59
  92.1 2.3 %copy-start.1 = (bf16[2048,128]{1,0:T(8,128)(2,1)S(1)}, bf16[2048,128]{1,0:T(8,128)(2,1)}, u32[]{:S(2)}) copy-start(bf16[2048,128]{1,0:T(8,128)(2,1)} %copy-done) | copy-start | bytes 1572868 | tf_op jit(solution)/shard_map/while
  101.0 2.8 %copy-start.1 = (bf16[2048,128]{1,0:T(8,128)(2,1)S(1)}, bf16[2048,128]{1,0:T(8,128)(2,1)}, u32[]{:S(2)}) copy-start(bf16[2048,128]{1,0:T(8,128)(2,1)} %copy-done) | copy-start | bytes 1572868 | tf_op jit(solution)/shard_map/while
  103.8 1.7 copy-start.2
  110.4 2.8 %copy-start.1 = (bf16[2048,128]{1,0:T(8,128)(2,1)S(1)}, bf16[2048,128]{1,0:T(8,128)(2,1)}, u32[]{:S(2)}) copy-start(bf16[2048,128]{1,0:T(8,128)(2,1)} %copy-done) | copy-start | bytes 1572868 | tf_op jit(solution)/shard_map/while
  113.2 1.7 copy-start.2
  119.7 2.8 %copy-start.1 = (bf16[2048,128]{1,0:T(8,128)(2,1)S(1)}, bf16[2048,128]{1,0:T(8,128)(2,1)}, u32[]{:S(2)}) copy-start(bf16[2048,128]{1,0:T(8,128)(2,1)} %copy-done) | copy-start | bytes 1572868 | tf_op jit(solution)/shard_map/while
  122.5 1.7 copy-start.2
  129.1 2.8 %copy-start.1 = (bf16[2048,128]{1,0:T(8,128)(2,1)S(1)}, bf16[2048,128]{1,0:T(8,128)(2,1)}, u32[]{:S(2)}) copy-start(bf16[2048,128]{1,0:T(8,128)(2,1)} %copy-done) | copy-start | bytes 1572868 | tf_op jit(solution)/shard_map/while
  131.9 1.7 copy-start.2
  138.4 2.8 %copy-start.1 = (bf16[2048,128]{1,0:T(8,128)(2,1)S(1)}, bf16[2048,128]{1,0:T(8,128)(2,1)}, u32[]{:S(2)}) copy-start(bf16[2048,128]{1,0:T(8,128)(2,1)} %copy-done) | copy-start | bytes 1572868 | tf_op jit(solution)/shard_map/while
  141.2 1.7 copy-start.2
  147.8 2.8 %copy-start.1 = (bf16[2048,128]{1,0:T(8,128)(2,1)S(1)}, bf16[2048,128]{1,0:T(8,128)(2,1)}, u32[]{:S(2)}) copy-start(bf16[2048,128]{1,0:T(8,128)(2,1)} %copy-done) | copy-start | bytes 1572868 | tf_op jit(solution)/shard_map/while
  150.6 1.7 copy-start.2
  157.1 2.8 %copy-start.1 = (bf16[2048,128]{1,0:T(8,128)(2,1)S(1)}, bf16[2048,128]{1,0:T(8,128)(2,1)}, u32[]{:S(2)}) copy-start(bf16[2048,128]{1,0:T(8,128)(2,1)} %copy-done) | copy-start | bytes 1572868 | tf_op jit(solution)/shard_map/while
  161.1 15.3 %collective-permute-start.3 = (f32[2,512,128]{2,1,0:T(8,128)S(1)}, f32[2,512,128]{2,1,0:T(8,128)S(1)}, u32[]{:S(2)}, u32[]{:S(2)}) collective-permute-start(f32[2,512,128]{2,1,0:T(8,128)S(1)} %get-tuple-element.398), channel_id=1, source_target_pairs={{1,0},{2,1},{3,2},{4,3},{5,4},{6,5},{7,6}} | collective-permute-start | bytes 1572872 | tf_op jit(solution)/shard_map/ppermute | solution.py:71
  163.5 16.8 %collective-permute-start.4 = (f32[2,512,128]{2,1,0:T(8,128)S(1)}, f32[2,512,128]{2,1,0:T(8,128)S(1)}, u32[]{:S(2)}, u32[]{:S(2)}) collective-permute-start(f32[2,512,128]{2,1,0:T(8,128)S(1)} %get-tuple-element.400), channel_id=1, source_target_pairs={{2,0},{3,1},{4,2},{5,3},{6,4},{7,5}} | collective-permute-start | bytes 1572872 | tf_op jit(solution)/shard_map/ppermute | solution.py:71
  166.7 28.3 %collective-permute-start.5 = (f32[2,512,128]{2,1,0:T(8,128)S(1)}, f32[2,512,128]{2,1,0:T(8,128)S(1)}, u32[]{:S(2)}, u32[]{:S(2)}) collective-permute-start(f32[2,512,128]{2,1,0:T(8,128)S(1)} %get-tuple-element.399), channel_id=1, source_target_pairs={{3,0},{4,1},{5,2},{6,3},{7,4}} | collective-permute-start | bytes 1572872 | tf_op jit(solution)/shard_map/ppermute | solution.py:71
  (10 other events, 16.6 us)
where the time goes:
time: 200 us; the launch traced here: 197 us
  other arithmetic  72.9 us (36%)
  matrix products  72 us (36%)
  waiting for transfers between devices  26.4 us (13%)
  starting transfers between devices  15.9 us (8%)
  local copies, waits for them, and re-layouts  8.47 us (4%)
    select_n x8, other arithmetic, doc_ids(): jnp.searchsorted(bounds[1:], positions, side='right').astype(jnp.int32)  66.1 us
    ppermute x3, waiting for transfers between devices, local(): lax.ppermute(part_sums[:, HOPS - hop], seq_axes, [(sender, sender - hop)...  26.4 us
    dot_general x8, matrix products, step(): jnp.einsum('qgk,qgd->kd', p_mat.astype(jnp.bfloat16), do_blk, preferred_e...  21.9 us
    dot_general x8, matrix products, step(): jnp.einsum('qgk,kd->qgd', ds_mat, k_win, preferred_element_type=jnp.float32)  16.2 us
    dot_general x8, matrix products, step(): jnp.einsum('qgk,qgd->kd', ds_mat, q_blk, preferred_element_type=jnp.float32)  13.2 us
    dot_general x8, matrix products, step(): jnp.einsum('qgd,kd->qgk', q_blk, k_win, preferred_element_type=jnp.float32)  11.2 us
    dot_general x8, matrix products, step(): jnp.einsum('qgd,kd->qgk', do_blk, v_win, preferred_element_type=jnp.float32)  9.42 us
    ppermute x3, starting transfers between devices, local(): lax.ppermute(kv_pair, seq_axes, [(sender, sender + hop) for sender in ran...  8.44 us
  transfers between devices with their start and end apart: 6, of which 3 were waited for; matrix products, arithmetic and copies ran while one was open for 38% of the time, Pallas kernels for 0%

commit v1 on v0

v1 whole, which is shorter than its diff:
```python
import functools
import math

import jax
import jax.numpy as jnp
from jax import lax
from jax.experimental import pallas as pl
from jax.experimental.pallas import tpu as pltpu
from jax.sharding import PartitionSpec as P

ROWS = 512
HEADS = 3
DIM = 128
CH = 128
NCH = ROWS // CH
NBOUND = 14
LOG2E = math.log2(math.e)
MESH = pl.DeviceIdType.MESH
F32 = jnp.float32
BF16 = jnp.bfloat16
NT = (((1,), (1,)), ((), ()))
TN = (((0,), (0,)), ((), ()))


def device(rank):
    return (0, rank // 4, lax.rem(rank, 4))


def kernel(cu_ref, q_hbm, k_hbm, v_hbm, o_hbm, lse_hbm, do_hbm, dq_ref, dk_ref, dv_ref,
           q_ref, do_ref, o_ref, lse_ref, drow, start_ref, kvown, kvx, kvl, dqt, own,
           mine, theirs, fromsib, xout, lret, xret, rly,
           in_sem, kv_s, kv_r, kx_s, kx_r, re_s, re_r, th_s, th_r, xo_s, xo_r, le_s, le_r, ry_s, ry_r):
    rank = lax.axis_index("cpo") * 4 + lax.axis_index("cp")
    core = lax.rem(rank, 2)
    chip = rank // 2
    sib = rank + 1 - 2 * core
    scale = DIM ** -0.5

    loads = [pltpu.make_async_copy(src, dst, in_sem.at[n]) for n, (src, dst) in enumerate([
        (k_hbm, kvown.at[0]), (v_hbm, kvown.at[1]), (do_hbm, do_ref), (o_hbm, o_ref), (q_hbm, q_ref), (lse_hbm, lse_ref)])]
    for copy in loads:
        copy.start()

    has_l = chip >= 1
    has_r = chip <= 2
    x_from = jnp.where(core == 1, rank - 1, rank - 3)
    x_to = jnp.where(core == 1, rank + 3, rank + 1)
    has_x = x_from >= 0
    x_ret = x_to <= 7

    barrier = pltpu.get_barrier_semaphore()

    def greet(other):
        pl.semaphore_signal(barrier, inc=1, device_id=device(other), device_id_type=MESH)

    greet(sib)
    pl.when(has_l)(lambda: greet(rank - 2))
    pl.when(has_r)(lambda: greet(rank + 2))
    pl.when((core == 1) & (chip <= 1))(lambda: greet(rank + 3))
    pl.when((core == 0) & (chip >= 2))(lambda: greet(rank - 3))
    pl.when(rank == 0)(lambda: greet(4))
    pl.when(rank == 4)(lambda: greet(0))
    one = jnp.int32(1)
    zero = jnp.int32(0)
    count = (one + jnp.where(has_l, one, zero) + jnp.where(has_r, one, zero)
             + jnp.where((core == 1) & (chip <= 1), one, zero) + jnp.where((core == 0) & (chip >= 2), one, zero)
             + jnp.where(rank == 0, one, zero) + jnp.where(rank == 4, one, zero))
    pl.semaphore_wait(barrier, count)

    def remote(src, dst, s_sem, r_sem, other):
        return pltpu.make_async_remote_copy(src_ref=src, dst_ref=dst, send_sem=s_sem, recv_sem=r_sem,
                                            device_id=device(other), device_id_type=MESH)

    def rows(i):
        return pl.ds(pl.multiple_of(i * CH, CH), CH)

    def kv_right(i):
        return remote(kvown.at[:, rows(i)], kvl.at[core, :, rows(i)], kv_s.at[i], kv_r.at[i], rank + 2)

    def kv_x(i):
        return remote(kvown.at[:, rows(i)], kvx.at[:, rows(i)], kx_s.at[i], kx_r.at[i], x_to)

    def kv_relay(i):
        return remote(kvl.at[core, :, rows(i)], kvl.at[core, :, rows(i)], re_s.at[i], re_r.at[i], sib)

    def kv_relayed(i):
        return remote(kvl.at[1 - core, :, rows(i)], kvl.at[1 - core, :, rows(i)], re_s.at[i], re_r.at[i], sib)

    def give_sib(i):
        return remote(theirs.at[i], fromsib.at[i], th_s.at[i], th_r.at[i], sib)

    def give_x(i):
        return remote(xout.at[i], xret.at[i], xo_s.at[i], xo_r.at[i], x_from)

    def give_left(i):
        return remote(mine.at[i], lret.at[i], le_s.at[i], le_r.at[i], rank - 2)

    def give_relay(i):
        return remote(mine.at[i], rly.at[i], le_s.at[i], ry_r.at[i], 0)

    def pass_on(i):
        return remote(rly.at[i], lret.at[i], ry_s.at[i], le_r.at[i], 2)

    loads[0].wait()
    loads[1].wait()

    def send_kv(i, _):
        pl.when(has_r)(lambda: kv_right(i).start())
        pl.when(x_ret)(lambda: kv_x(i).start())
        return 0

    lax.fori_loop(0, NCH, send_kv, 0)

    pos = rank * ROWS + lax.broadcasted_iota(jnp.int32, (1, ROWS), 1)
    start = jnp.zeros((1, ROWS), jnp.int32)
    for n in range(NBOUND):
        bound = cu_ref[n]
        start = jnp.where(bound <= pos, bound, start)
    start_ref[0:1, :] = start

    loads[2].wait()
    loads[3].wait()
    for g in range(HEADS):
        prod = do_ref[g].astype(F32) * o_ref[g].astype(F32)
        drow[g:g + 1, :] = jnp.sum(prod.T, axis=0, keepdims=True)
    loads[4].wait()
    loads[5].wait()

    def part(kv, i, first_key, diag):
        k = kv[0, rows(i), :]
        v = kv[1, rows(i), :]
        key = first_key + i * CH + lax.broadcasted_iota(jnp.int32, (CH, ROWS), 0)
        keep = key >= start_ref[0:1, :]
        if diag:
            keep = keep & (key <= rank * ROWS + lax.broadcasted_iota(jnp.int32, (CH, ROWS), 1))
        dk = dv = None
        for g in range(HEADS):
            q, do = q_ref[g], do_ref[g]
            s = lax.dot_general(k, q, NT, preferred_element_type=F32)
            p = jnp.exp2(s * (scale * LOG2E) - lse_ref[g:g + 1, :] * LOG2E)
            p = jnp.where(keep, p, 0.0)
            dp = lax.dot_general(v, do, NT, preferred_element_type=F32)
            ds = (p * (dp - drow[g:g + 1, :])).astype(BF16)
            dv_g = jnp.dot(p.astype(BF16), do, preferred_element_type=F32)
            dk_g = jnp.dot(ds, q, preferred_element_type=F32)
            dk, dv = (dk_g, dv_g) if dk is None else (dk + dk_g, dv + dv_g)
            dqt[g] += lax.dot_general(k, ds, TN, preferred_element_type=F32)
        return dk, dv

    dqt[...] = jnp.zeros_like(dqt)

    def diag_step(i, _):
        dk, dv = part(kvown, i, rank * ROWS, True)
        own[i, 0] = dk
        own[i, 1] = dv
        return 0

    lax.fori_loop(0, NCH, diag_step, 0)

    def step(i, _):
        @pl.when(has_l)
        def _():
            kv_right(i).wait_recv()
            kv_relay(i).start()
            dk, dv = part(kvl.at[core], i, (rank - 2) * ROWS, False)
            mine[i, 0] = dk
            mine[i, 1] = dv
            kv_relayed(i).wait_recv()
            dk, dv = part(kvl.at[1 - core], i, (sib - 2) * ROWS, False)
            theirs[i, 0] = dk
            theirs[i, 1] = dv
            give_sib(i).start()

        @pl.when(has_x)
        def _():
            kv_x(i).wait_recv()
            dk, dv = part(kvx, i, x_from * ROWS, False)
            xout[i, 0] = dk
            xout[i, 1] = dv
            give_x(i).start()

        @pl.when(has_l)
        def _():
            give_sib(i).wait_recv()
            mine[i] += fromsib[i]
            pl.when(rank != 4)(lambda: give_left(i).start())
            pl.when(rank == 4)(lambda: give_relay(i).start())

        return 0

    lax.fori_loop(0, NCH, step, 0)

    @pl.when(rank == 0)
    def _():
        def fwd(i, _):
            give_relay(i).wait_recv()
            pass_on(i).start()
            return 0
        lax.fori_loop(0, NCH, fwd, 0)

    for g in range(HEADS):
        dq_ref[g] = (dqt[g].T * scale).astype(BF16)

    def finish(i, _):
        @pl.when(x_ret)
        def _():
            give_x(i).wait_recv()
            own[i] += xret[i]

        @pl.when(has_r)
        def _():
            give_left(i).wait_recv()
            own[i] += lret[i]

        dk_ref[rows(i), :] = (own[i, 0] * scale).astype(BF16)
        dv_ref[rows(i), :] = own[i, 1].astype(BF16)
        return 0

    lax.fori_loop(0, NCH, finish, 0)

    def drain(i, _):
        pl.when(has_r)(lambda: kv_right(i).wait_send())
        pl.when(x_ret)(lambda: kv_x(i).wait_send())

        @pl.when(has_l)
        def _():
            kv_relay(i).wait_send()
            give_sib(i).wait_send()
            give_left(i).wait_send()

        pl.when(has_x)(lambda: give_x(i).wait_send())
        pl.when(rank == 0)(lambda: pass_on(i).wait_send())
        return 0

    lax.fori_loop(0, NCH, drain, 0)


def solution(mesh):
    def local(queries, keys, values, attn_out, logsumexp, d_out, cu_seqlens):
        rows, heads, head = queries.shape
        swap = lambda a: jnp.transpose(a, (1, 0, 2))
        big = pltpu.VMEM((heads, rows, head), BF16)
        kv = pltpu.VMEM((2, rows, head), BF16)
        sums = pltpu.VMEM((NCH, 2, CH, head), F32)
        sem = pltpu.SemaphoreType.DMA((NCH,))
        anyspec = pl.BlockSpec(memory_space=pl.ANY)
        vspec = pl.BlockSpec(memory_space=pltpu.VMEM)
        dq, dk, dv = pl.pallas_call(
            kernel,
            out_shape=(jax.ShapeDtypeStruct((heads, rows, head), BF16),
                       jax.ShapeDtypeStruct((rows, head), BF16),
                       jax.ShapeDtypeStruct((rows, head), BF16)),
            in_specs=[pl.BlockSpec(memory_space=pltpu.SMEM)] + [anyspec] * 6,
            out_specs=(vspec, vspec, vspec),
            scratch_shapes=[big, big, big, pltpu.VMEM((heads, rows), F32), pltpu.VMEM((8, rows), F32),
                            pltpu.VMEM((8, rows), jnp.int32), kv, kv, pltpu.VMEM((2, 2, rows, head), BF16),
                            pltpu.VMEM((heads, head, rows), F32), sums,
                            sums, sums, sums, sums, sums, sums, sums,
                            pltpu.SemaphoreType.DMA((6,))] + [sem] * 14,
            compiler_params=pltpu.CompilerParams(collective_id=0, has_side_effects=True,
                                                 vmem_limit_bytes=48 << 20),
        )(cu_seqlens, swap(queries), keys, values, swap(attn_out), logsumexp.T, swap(d_out))
        return jnp.transpose(dq, (1, 0, 2)), dk, dv

    seq = P(("dp", "cpo", "cp"))
    return jax.shard_map(local, mesh=mesh, in_specs=(seq,) * 6 + (P("dp"),), out_specs=(seq, seq, seq), check_vma=False)
```

time: 200 us -> 40 us (0.20)
  the two profiles are of different devices: /device:TPU:3 before, /device:TPU:0 now
where the time goes in v1:
time: 40 us; the launch traced here: 39.7 us
  Pallas kernels  30.9 us (77%)
  local copies, waits for them, and re-layouts  8.2 us (20%)
  between operations  0.66 us (2%)
    pallas_call x1, Pallas kernels, local(): pl.pallas_call(kernel, out_shape=(jax.ShapeDtypeStruct((heads, rows, head...  30.9 us
    unnamed x17, local copies, waits for them, and re-layouts  8.2 us

profile of v1, /device:TPU:0, one launch (start us, length us, event | category | flops | bytes accessed | tf_op | source)
XLA Modules:
  0.0 39.7 jit_solution(5713027184483053693)
XLA Ops:
  0.6 0.0 copy-start.6
  0.6 0.6 %copy-done.6 = s32[14]{0:T(128)S(1)} copy-done((s32[14]{0:T(128)S(1)}, s32[14]{0:T(128)}, u32[]{:S(2)}) %copy-start.6) | copy-done | bytes 80
  1.3 0.0 copy-start
  1.3 1.0 %copy-done = bf16[512,3,128]{2,0,1:T(8,128)(2,1)S(1)} copy-done((bf16[512,3,128]{2,0,1:T(8,128)(2,1)S(1)}, bf16[512,3,128]{2,0,1:T(8,128)(2,1)}, u32[]{:S(2)}) %copy-start) | copy-done | bytes 393240
  2.3 0.0 copy-start.1
  2.3 1.0 %copy-done.1 = bf16[512,3,128]{2,0,1:T(8,128)(2,1)S(1)} copy-done((bf16[512,3,128]{2,0,1:T(8,128)(2,1)S(1)}, bf16[512,3,128]{2,0,1:T(8,128)(2,1)}, u32[]{:S(2)}) %copy-start.1) | copy-done | bytes 393240
  3.3 0.0 copy-start.2
  3.3 1.0 %copy-done.2 = bf16[512,3,128]{2,0,1:T(8,128)(2,1)S(1)} copy-done((bf16[512,3,128]{2,0,1:T(8,128)(2,1)S(1)}, bf16[512,3,128]{2,0,1:T(8,128)(2,1)}, u32[]{:S(2)}) %copy-start.2) | copy-done | bytes 393240
  4.3 0.0 copy-start.3
  4.3 0.9 %copy-done.3 = bf16[512,128]{1,0:T(8,128)(2,1)S(1)} copy-done((bf16[512,128]{1,0:T(8,128)(2,1)S(1)}, bf16[512,128]{1,0:T(8,128)(2,1)}, u32[]{:S(2)}) %copy-start.3) | copy-done | bytes 131096
  5.2 0.0 copy-start.4
  5.2 0.9 %copy-done.4 = bf16[512,128]{1,0:T(8,128)(2,1)S(1)} copy-done((bf16[512,128]{1,0:T(8,128)(2,1)S(1)}, bf16[512,128]{1,0:T(8,128)(2,1)}, u32[]{:S(2)}) %copy-start.4) | copy-done | bytes 131096
  6.1 0.0 copy-start.5
  6.1 0.7 %copy-done.5 = f32[512,3]{0,1:T(4,128)S(1)} copy-done((f32[512,3]{0,1:T(4,128)S(1)}, f32[512,3]{0,1:T(4,128)}, u32[]{:S(2)}) %copy-start.5) | copy-done | bytes 6168
  6.8 30.9 %shard_map.94 = (bf16[3,512,128]{2,1,0:T(8,128)(2,1)S(1)}, bf16[512,128]{1,0:T(8,128)(2,1)S(1)}, bf16[512,128]{1,0:T(8,128)(2,1)S(1)}) custom-call(s32[14]{0:T(128)S(1)} %copy-done.6, bf16[3,512,128]{2,1,0:T(8,128)(2,1)S(1)} %bitcast.6, bf16[512,128]{1,0:T(8,128)(2,1)S(1)} %copy-done.3, bf16[512,128]{1,0:T(8,128)(2,1)S(1)} %copy-done.4, ...), custom_call_target="tpu_custom_call" | custom-call | tf_op jit(solution)/shard_map/pallas_call | solution.py:248
  37.7 0.7 %copy.13 = bf16[512,3,128]{2,0,1:T(8,128)(2,1)} copy(bf16[512,3,128]{2,0,1:T(8,128)(2,1)S(1)} %bitcast.5) | data formatting | bytes 786432
  38.4 0.7 %copy.14 = bf16[512,128]{1,0:T(8,128)(2,1)} copy(bf16[512,128]{1,0:T(8,128)(2,1)S(1)} %get-tuple-element.13) | data formatting | bytes 262144
  39.1 0.7 %copy.15 = bf16[512,128]{1,0:T(8,128)(2,1)} copy(bf16[512,128]{1,0:T(8,128)(2,1)S(1)} %get-tuple-element.14) | data formatting | bytes 262144
Async XLA Ops:
  0.6 0.7 %copy-start.6 = (s32[14]{0:T(128)S(1)}, s32[14]{0:T(128)}, u32[]{:S(2)}) copy-start(s32[14]{0:T(128)} %cu_ref.1) | copy-start | bytes 172
  1.3 1.0 %copy-start = (bf16[512,3,128]{2,0,1:T(8,128)(2,1)S(1)}, bf16[512,3,128]{2,0,1:T(8,128)(2,1)}, u32[]{:S(2)}) copy-start(bf16[512,3,128]{2,0,1:T(8,128)(2,1)} %param.7) | copy-start | bytes 1179652
  2.3 1.0 %copy-start.1 = (bf16[512,3,128]{2,0,1:T(8,128)(2,1)S(1)}, bf16[512,3,128]{2,0,1:T(8,128)(2,1)}, u32[]{:S(2)}) copy-start(bf16[512,3,128]{2,0,1:T(8,128)(2,1)} %param.10) | copy-start | bytes 1179652
  3.3 1.0 %copy-start.2 = (bf16[512,3,128]{2,0,1:T(8,128)(2,1)S(1)}, bf16[512,3,128]{2,0,1:T(8,128)(2,1)}, u32[]{:S(2)}) copy-start(bf16[512,3,128]{2,0,1:T(8,128)(2,1)} %param.12) | copy-start | bytes 1179652
  4.3 0.9 %copy-start.3 = (bf16[512,128]{1,0:T(8,128)(2,1)S(1)}, bf16[512,128]{1,0:T(8,128)(2,1)}, u32[]{:S(2)}) copy-start(bf16[512,128]{1,0:T(8,128)(2,1)} %k_hbm.1) | copy-start | bytes 393220
  5.2 0.9 %copy-start.4 = (bf16[512,128]{1,0:T(8,128)(2,1)S(1)}, bf16[512,128]{1,0:T(8,128)(2,1)}, u32[]{:S(2)}) copy-start(bf16[512,128]{1,0:T(8,128)(2,1)} %v_hbm.1) | copy-start | bytes 393220
  6.1 0.7 %copy-start.5 = (f32[512,3]{0,1:T(4,128)S(1)}, f32[512,3]{0,1:T(4,128)}, u32[]{:S(2)}) copy-start(f32[512,3]{0,1:T(4,128)} %param.11) | copy-start | bytes 18436

commit v2 on v1

--- a/solution.py
+++ b/solution.py
@@ -14,6 +14,7 @@
 CH = 128
 NCH = ROWS // CH
 NBOUND = 14
+QALL = HEADS * ROWS
 LOG2E = math.log2(math.e)
 MESH = pl.DeviceIdType.MESH
 F32 = jnp.float32
@@ -23,23 +24,18 @@
 
 
 def device(rank):
-    return (0, rank // 4, lax.rem(rank, 4))
-
-
-def kernel(cu_ref, q_hbm, k_hbm, v_hbm, o_hbm, lse_hbm, do_hbm, dq_ref, dk_ref, dv_ref,
-           q_ref, do_ref, o_ref, lse_ref, drow, start_ref, kvown, kvx, kvl, dqt, own,
+    return (0, rank >> 2, rank & 3)
+
+
+def kernel(cu_hbm, q_hbm, k_hbm, v_hbm, o_hbm, lse_hbm, do_hbm, dq_ref, dk_ref, dv_ref,
+           cu_ref, q_ref, do_ref, o_ref, lse_ref, lrow, drow, start_ref, kvown, kvx, kvl, dqt, own,
            mine, theirs, fromsib, xout, lret, xret, rly,
            in_sem, kv_s, kv_r, kx_s, kx_r, re_s, re_r, th_s, th_r, xo_s, xo_r, le_s, le_r, ry_s, ry_r):
     rank = lax.axis_index("cpo") * 4 + lax.axis_index("cp")
-    core = lax.rem(rank, 2)
-    chip = rank // 2
+    core = rank & 1
+    chip = rank >> 1
     sib = rank + 1 - 2 * core
     scale = DIM ** -0.5
-
-    loads = [pltpu.make_async_copy(src, dst, in_sem.at[n]) for n, (src, dst) in enumerate([
-        (k_hbm, kvown.at[0]), (v_hbm, kvown.at[1]), (do_hbm, do_ref), (o_hbm, o_ref), (q_hbm, q_ref), (lse_hbm, lse_ref)])]
-    for copy in loads:
-        copy.start()
 
     has_l = chip >= 1
     has_r = chip <= 2
@@ -60,6 +56,11 @@
     pl.when((core == 0) & (chip >= 2))(lambda: greet(rank - 3))
     pl.when(rank == 0)(lambda: greet(4))
     pl.when(rank == 4)(lambda: greet(0))
+    loads = [pltpu.make_async_copy(src, dst, in_sem.at[n]) for n, (src, dst) in enumerate([
+        (k_hbm, kvown.at[0]), (v_hbm, kvown.at[1]), (do_hbm, do_ref), (o_hbm, o_ref), (q_hbm, q_ref), (lse_hbm, lse_ref), (cu_hbm, cu_ref)])]
+    for copy in loads:
+        copy.start()
+
     one = jnp.int32(1)
     zero = jnp.int32(0)
     count = (one + jnp.where(has_l, one, zero) + jnp.where(has_r, one, zero)
@@ -113,38 +114,38 @@
 
     pos = rank * ROWS + lax.broadcasted_iota(jnp.int32, (1, ROWS), 1)
     start = jnp.zeros((1, ROWS), jnp.int32)
+    loads[6].wait()
     for n in range(NBOUND):
         bound = cu_ref[n]
         start = jnp.where(bound <= pos, bound, start)
-    start_ref[0:1, :] = start
 
     loads[2].wait()
     loads[3].wait()
+    loads[5].wait()
     for g in range(HEADS):
-        prod = do_ref[g].astype(F32) * o_ref[g].astype(F32)
-        drow[g:g + 1, :] = jnp.sum(prod.T, axis=0, keepdims=True)
+        lanes = slice(g * ROWS, (g + 1) * ROWS)
+        prod = do_ref[lanes].astype(F32) * o_ref[lanes].astype(F32)
+        drow[0:1, lanes] = jnp.sum(prod.T, axis=0, keepdims=True)
+        lrow[0:1, lanes] = lse_ref[g:g + 1, :] * LOG2E
+        start_ref[0:1, lanes] = start
     loads[4].wait()
-    loads[5].wait()
 
     def part(kv, i, first_key, diag):
         k = kv[0, rows(i), :]
         v = kv[1, rows(i), :]
-        key = first_key + i * CH + lax.broadcasted_iota(jnp.int32, (CH, ROWS), 0)
+        q, do = q_ref[...], do_ref[...]
+        key = first_key + i * CH + lax.broadcasted_iota(jnp.int32, (CH, QALL), 0)
         keep = key >= start_ref[0:1, :]
         if diag:
-            keep = keep & (key <= rank * ROWS + lax.broadcasted_iota(jnp.int32, (CH, ROWS), 1))
-        dk = dv = None
-        for g in range(HEADS):
-            q, do = q_ref[g], do_ref[g]
-            s = lax.dot_general(k, q, NT, preferred_element_type=F32)
-            p = jnp.exp2(s * (scale * LOG2E) - lse_ref[g:g + 1, :] * LOG2E)
-            p = jnp.where(keep, p, 0.0)
-            dp = lax.dot_general(v, do, NT, preferred_element_type=F32)
-            ds = (p * (dp - drow[g:g + 1, :])).astype(BF16)
-            dv_g = jnp.dot(p.astype(BF16), do, preferred_element_type=F32)
-            dk_g = jnp.dot(ds, q, preferred_element_type=F32)
-            dk, dv = (dk_g, dv_g) if dk is None else (dk + dk_g, dv + dv_g)
-            dqt[g] += lax.dot_general(k, ds, TN, preferred_element_type=F32)
+            keep = keep & (key - rank * ROWS <= lax.rem(lax.broadcasted_iota(jnp.int32, (CH, QALL), 1), ROWS))
+        s = lax.dot_general(k, q, NT, preferred_element_type=F32)
+        dp = lax.dot_general(v, do, NT, preferred_element_type=F32)
+        p = jnp.exp2(s * (scale * LOG2E) - lrow[0:1, :])
+        p = jnp.where(keep, p, 0.0)
+        ds = (p * (dp - drow[0:1, :])).astype(BF16)
+        dv = jnp.dot(p.astype(BF16), do, preferred_element_type=F32)
+        dk = jnp.dot(ds, q, preferred_element_type=F32)
+        dqt[...] += lax.dot_general(k, ds, TN, preferred_element_type=F32)
         return dk, dv
 
     dqt[...] = jnp.zeros_like(dqt)
@@ -157,38 +158,44 @@
 
     lax.fori_loop(0, NCH, diag_step, 0)
 
-    def step(i, _):
-        @pl.when(has_l)
-        def _():
-            kv_right(i).wait_recv()
-            kv_relay(i).start()
-            dk, dv = part(kvl.at[core], i, (rank - 2) * ROWS, False)
-            mine[i, 0] = dk
-            mine[i, 1] = dv
+    @pl.when(has_l)
+    def _():
+        kv_right(0).wait_recv()
+        kv_relay(0).start()
+
+        def step(i, _):
             kv_relayed(i).wait_recv()
             dk, dv = part(kvl.at[1 - core], i, (sib - 2) * ROWS, False)
             theirs[i, 0] = dk
             theirs[i, 1] = dv
             give_sib(i).start()
 
-        @pl.when(has_x)
-        def _():
+            @pl.when(i + 1 < NCH)
+            def _():
+                kv_right(i + 1).wait_recv()
+                kv_relay(i + 1).start()
+
+            dk, dv = part(kvl.at[core], i, (rank - 2) * ROWS, False)
+            give_sib(i).wait_recv()
+            mine[i, 0] = dk + fromsib[i, 0]
+            mine[i, 1] = dv + fromsib[i, 1]
+            pl.when(rank != 4)(lambda: give_left(i).start())
+            pl.when(rank == 4)(lambda: give_relay(i).start())
+            return 0
+
+        lax.fori_loop(0, NCH, step, 0)
+
+    @pl.when(has_x)
+    def _():
+        def xstep(i, _):
             kv_x(i).wait_recv()
             dk, dv = part(kvx, i, x_from * ROWS, False)
             xout[i, 0] = dk
             xout[i, 1] = dv
             give_x(i).start()
-
-        @pl.when(has_l)
-        def _():
-            give_sib(i).wait_recv()
-            mine[i] += fromsib[i]
-            pl.when(rank != 4)(lambda: give_left(i).start())
-            pl.when(rank == 4)(lambda: give_relay(i).start())
-
-        return 0
-
-    lax.fori_loop(0, NCH, step, 0)
+            return 0
+
+        lax.fori_loop(0, NCH, xstep, 0)
 
     @pl.when(rank == 0)
     def _():
@@ -199,7 +206,8 @@
         lax.fori_loop(0, NCH, fwd, 0)
 
     for g in range(HEADS):
-        dq_ref[g] = (dqt[g].T * scale).astype(BF16)
+        lanes = slice(g * ROWS, (g + 1) * ROWS)
+        dq_ref[lanes] = (dqt[:, lanes].T * scale).astype(BF16)
 
     def finish(i, _):
         @pl.when(x_ret)
@@ -235,11 +243,20 @@
     lax.fori_loop(0, NCH, drain, 0)
 
 
+def write_out(dq_ref, dk_ref, dv_ref, dq_hbm, dk_hbm, dv_hbm, sem):
+    copies = [pltpu.make_async_copy(src, dst, sem.at[n]) for n, (src, dst) in enumerate([
+        (dq_ref, dq_hbm), (dk_ref, dk_hbm), (dv_ref, dv_hbm)])]
+    for copy in copies:
+        copy.start()
+    for copy in copies:
+        copy.wait()
+
+
 def solution(mesh):
     def local(queries, keys, values, attn_out, logsumexp, d_out, cu_seqlens):
         rows, heads, head = queries.shape
-        swap = lambda a: jnp.transpose(a, (1, 0, 2))
-        big = pltpu.VMEM((heads, rows, head), BF16)
+        swap = lambda a: jnp.transpose(a, (1, 0, 2)).reshape(heads * rows, head)
+        big = pltpu.VMEM((QALL, head), BF16)
         kv = pltpu.VMEM((2, rows, head), BF16)
         sums = pltpu.VMEM((NCH, 2, CH, head), F32)
         sem = pltpu.SemaphoreType.DMA((NCH,))
@@ -247,20 +264,28 @@
         vspec = pl.BlockSpec(memory_space=pltpu.VMEM)
         dq, dk, dv = pl.pallas_call(
             kernel,
-            out_shape=(jax.ShapeDtypeStruct((heads, rows, head), BF16),
-                       jax.ShapeDtypeStruct((rows, head), BF16),
-                       jax.ShapeDtypeStruct((rows, head), BF16)),
-            in_specs=[pl.BlockSpec(memory_space=pltpu.SMEM)] + [anyspec] * 6,
+            out_shape=(pltpu.VMEM((QALL, head), BF16), pltpu.VMEM((rows, head), BF16), pltpu.VMEM((rows, head), BF16)),
+            in_specs=[anyspec] * 7,
             out_specs=(vspec, vspec, vspec),
-            scratch_shapes=[big, big, big, pltpu.VMEM((heads, rows), F32), pltpu.VMEM((8, rows), F32),
-                            pltpu.VMEM((8, rows), jnp.int32), kv, kv, pltpu.VMEM((2, 2, rows, head), BF16),
-                            pltpu.VMEM((heads, head, rows), F32), sums,
+            scratch_shapes=[pltpu.SMEM((NBOUND,), jnp.int32), big, big, big, pltpu.VMEM((heads, rows), F32), pltpu.VMEM((8, QALL), F32),
+                            pltpu.VMEM((8, QALL), F32), pltpu.VMEM((8, QALL), jnp.int32), kv, kv, pltpu.VMEM((2, 2, rows, head), BF16),
+                            pltpu.VMEM((head, QALL), F32), sums,
                             sums, sums, sums, sums, sums, sums, sums,
-                            pltpu.SemaphoreType.DMA((6,))] + [sem] * 14,
+                            pltpu.SemaphoreType.DMA((7,))] + [sem] * 14,
             compiler_params=pltpu.CompilerParams(collective_id=0, has_side_effects=True,
                                                  vmem_limit_bytes=48 << 20),
-        )(cu_seqlens, swap(queries), keys, values, swap(attn_out), logsumexp.T, swap(d_out))
-        return jnp.transpose(dq, (1, 0, 2)), dk, dv
+        )(*[pltpu.with_memory_space_constraint(a, pltpu.HBM) for a in (
+            cu_seqlens, swap(queries), keys, values, swap(attn_out), logsumexp.T, swap(d_out))])
+        dq, dk, dv = pl.pallas_call(
+            write_out,
+            out_shape=(jax.ShapeDtypeStruct(dq.shape, BF16), jax.ShapeDtypeStruct(dk.shape, BF16),
+                       jax.ShapeDtypeStruct(dv.shape, BF16)),
+            in_specs=[vspec] * 3,
+            out_specs=(anyspec,) * 3,
+            scratch_shapes=[pltpu.SemaphoreType.DMA((3,))],
+            compiler_params=pltpu.CompilerParams(vmem_limit_bytes=4 << 20),
+        )(dq, dk, dv)
+        return jnp.transpose(dq.reshape(heads, rows, head), (1, 0, 2)), dk, dv
 
     seq = P(("dp", "cpo", "cp"))
     return jax.shard_map(local, mesh=mesh, in_specs=(seq,) * 6 + (P("dp"),), out_specs=(seq, seq, seq), check_vma=False)

time: 40 us -> 28 us (0.70)
  the two profiles are of different devices: /device:TPU:0 before, /device:TPU:1 now
where the time goes in v2:
time: 28 us; the launch traced here: 27.9 us
  Pallas kernels  27.2 us (97%)
  between operations  0.64 us (2%)
    pallas_call x1, Pallas kernels, local(): pl.pallas_call(kernel, out_shape=(pltpu.VMEM((QALL, head), BF16), pltpu.V...  26.4 us
    pallas_call x1, Pallas kernels, local(): pl.pallas_call(write_out, out_shape=(jax.ShapeDtypeStruct(dq.shape, BF16)...  0.86 us

profile of v2, /device:TPU:1, one launch (start us, length us, event | category | flops | bytes accessed | tf_op | source)
XLA Modules:
  0.0 27.9 jit_solution(13136631641236917752)
XLA Ops:
  0.6 26.4 %shard_map.94 = (bf16[1536,128]{1,0:T(8,128)(2,1)S(1)}, bf16[512,128]{1,0:T(8,128)(2,1)S(1)}, bf16[512,128]{1,0:T(8,128)(2,1)S(1)}) custom-call(s32[14]{0:T(128)} %cu_hbm.1, bf16[1536,128]{1,0:T(8,128)(2,1)} %bitcast.13, bf16[512,128]{1,0:T(8,128)(2,1)} %k_hbm.1, bf16[512,128]{1,0:T(8,128)(2,1)} %v_hbm.1, bf16[1536,128]{1,0:T(8,128)(2,1)} %bitcast.14, ...), custom_call_target="tpu_custom_call" | custom-call | tf_op jit(solution)/shard_map/pallas_call | solution.py:265
  27.0 0.9 %shard_map.95 = (bf16[1536,128]{1,0:T(8,128)(2,1)}, bf16[512,128]{1,0:T(8,128)(2,1)}, bf16[512,128]{1,0:T(8,128)(2,1)}) custom-call(bf16[1536,128]{1,0:T(8,128)(2,1)S(1)} %get-tuple-element.9.dq_ref, bf16[512,128]{1,0:T(8,128)(2,1)S(1)} %get-tuple-element.10.dk_ref, bf16[512,128]{1,0:T(8,128)(2,1)S(1)} %get-tuple-element.11.dv_ref), custom_call_target="tpu_custom_call" | custom-call | tf_op jit(solution)/shard_map/pallas_call | solution.py:279

commit v3 on v2

v3 whole, which is shorter than its diff:
```python
import math

import jax
import jax.numpy as jnp
from jax import lax
from jax.experimental import pallas as pl
from jax.experimental.pallas import tpu as pltpu
from jax.sharding import PartitionSpec as P

ROWS = 512
HEADS = 3
DIM = 128
NBOUND = 14
QALL = HEADS * ROWS
XCH = 256
NX = ROWS // XCH
LSIZE = (64, 64, 128, 128, 128)
LOFF = (0, 64, 128, 256, 384)
NL = len(LSIZE)
NRLY = 4
STEPS = tuple(zip(LOFF, LSIZE))
LOG2E = math.log2(math.e)
MESH = pl.DeviceIdType.MESH
F32 = jnp.float32
BF16 = jnp.bfloat16
NT = (((1,), (1,)), ((), ()))
TN = (((0,), (0,)), ((), ()))


def device(rank):
    return (0, rank >> 2, rank & 3)


def kernel(cu_hbm, q_hbm, k_hbm, v_hbm, o_hbm, lse_hbm, do_hbm, dq_ref, dk_ref, dv_ref,
           cu_ref, qd, row, qfar, rfar, o_ref, lse_ref, kvown, kvx, kvl, kvb, dqt, own, mine, xout, lret, xret, rly,
           in_sem, sb_s, sb_r, kv_s, kv_r, re_s, re_r, le_s, le_r, ry_s, ry_r, kx_s, kx_r, xo_s, xo_r, bn_s, bn_r):
    rank = lax.axis_index("cpo") * 4 + lax.axis_index("cp")
    core = rank & 1
    chip = rank >> 1
    sib = rank + 1 - 2 * core
    scale = DIM ** -0.5

    loads = [pltpu.make_async_copy(src, dst, in_sem.at[n]) for n, (src, dst) in enumerate([
        (k_hbm, kvown.at[0]), (v_hbm, kvown.at[1]), (do_hbm, qd.at[0, 1]), (q_hbm, qd.at[0, 0]), (o_hbm, o_ref),
        (lse_hbm, lse_ref), (cu_hbm, cu_ref)])]
    loads[0].start()
    loads[1].start()

    has_l = chip >= 1
    has_r = chip <= 2
    x_from = jnp.where(core == 1, rank - 1, rank - 3)
    x_to = jnp.where(core == 1, rank + 3, rank + 1)
    has_x = x_from >= 0
    x_ret = x_to <= 7

    barrier = pltpu.get_barrier_semaphore()

    def greet(other):
        pl.semaphore_signal(barrier, inc=1, device_id=device(other), device_id_type=MESH)

    far_right = (core == 1) & (chip <= 1)
    far_left = (core == 0) & (chip >= 2)
    pl.when(has_l)(lambda: greet(rank - 2))
    pl.when(has_r)(lambda: greet(rank + 2))
    pl.when(far_right)(lambda: greet(rank + 3))
    pl.when(far_left)(lambda: greet(rank - 3))
    pl.when(chip == 1)(lambda: greet(rank + 4))
    pl.when(chip == 3)(lambda: greet(rank - 4))
    pl.when(rank == 0)(lambda: greet(4))
    pl.when(rank == 4)(lambda: greet(0))
    greet(sib)
    for copy in loads[2:]:
        copy.start()
    one = jnp.int32(1)
    zero = jnp.int32(0)
    count = one
    for there in (has_l, has_r, far_right, far_left, chip == 1, chip == 3, rank == 0, rank == 4):
        count = count + jnp.where(there, one, zero)
    pl.semaphore_wait(barrier, count)

    def remote(src, dst, s_sem, r_sem, other):
        return pltpu.make_async_remote_copy(src_ref=src, dst_ref=dst, send_sem=s_sem, recv_sem=r_sem,
                                            device_id=device(other), device_id_type=MESH)

    def rows(off, size):
        return pl.ds(off, size)

    def lend(src, dst, n, other):
        return remote(src, dst, sb_s.at[n], sb_r.at[n], other)

    def kv_right(i, off, size):
        return remote(kvown.at[:, rows(off, size)], kvl.at[core, :, rows(off, size)], kv_s.at[i], kv_r.at[i], rank + 2)

    last = pl.ds(LOFF[-1], LSIZE[-1])

    def bounce():
        return remote(kvown.at[:, last], kvb, kv_s.at[NL - 1], bn_r.at[0], rank + 4)

    def bounce_on():
        return remote(kvb, kvl.at[core, :, last], bn_s.at[0], kv_r.at[NL - 1], rank - 2)

    def kv_relay(i, off, size):
        return remote(kvl.at[core, :, rows(off, size)], kvl.at[core, :, rows(off, size)], re_s.at[i], re_r.at[i], sib)

    def kv_relayed(i, off, size):
        part = kvl.at[1 - core, :, rows(off, size)]
        return remote(part, part, re_s.at[i], re_r.at[i], sib)

    def kv_x(i):
        return remote(kvown.at[:, rows(i * XCH, XCH)], kvx.at[:, rows(i * XCH, XCH)], kx_s.at[i], kx_r.at[i], x_to)

    def give_x():
        return remote(xout, xret, xo_s.at[0], xo_r.at[0], rank - 3)

    def give_left(i, off, size):
        return remote(mine.at[:, rows(off, size)], lret.at[:, rows(off, size)], le_s.at[i], le_r.at[i], rank - 2)

    def give_relay(i, off, size):
        return remote(mine.at[:, rows(off, size)], rly.at[:, rows(off, size)], le_s.at[i], ry_r.at[i], 0)

    def pass_on(i, off, size):
        return remote(rly.at[:, rows(off, size)], lret.at[:, rows(off, size)], ry_s.at[i], le_r.at[i], 2)

    loads[0].wait()
    loads[1].wait()

    @pl.when(has_r)
    def _():
        pl.when(chip == 1)(lambda: bounce().start())
        for i in range(NL - 1):
            kv_right(i, LOFF[i], LSIZE[i]).start()
        pl.when(chip != 1)(lambda: kv_right(NL - 1, LOFF[-1], LSIZE[-1]).start())

    loads[2].wait()
    loads[3].wait()
    sib_qd, sib_row = lend(qd.at[0], qd.at[1], 0, sib), lend(row.at[0], row.at[1], 1, sib)
    far_to = jnp.where(core == 0, rank - 3, rank + 3)
    far_qd, far_row = lend(qd.at[0, :, :, 0:XCH], qfar, 2, far_to), lend(rfar.at[0], rfar.at[1], 3, far_to)
    sib_qd.start()
    pl.when(far_left)(lambda: far_qd.start())

    pos = rank * ROWS + lax.broadcasted_iota(jnp.int32, (1, ROWS), 1)
    start = jnp.zeros((1, ROWS), jnp.int32)
    loads[6].wait()
    for n in range(NBOUND):
        bound = cu_ref[n]
        start = jnp.where(bound <= pos, bound, start)
    loads[4].wait()
    loads[5].wait()
    for g in range(HEADS):
        lanes = slice(g * ROWS, (g + 1) * ROWS)
        prod = qd[0, 1, g].astype(F32) * o_ref[g].astype(F32)
        half = slice(g * XCH, (g + 1) * XCH)
        for n, line in enumerate([lse_ref[g:g + 1, :] * LOG2E, jnp.sum(prod.T, axis=0, keepdims=True), start.astype(F32)]):
            row[0, n:n + 1, lanes] = line
            rfar[0, n:n + 1, half] = line[:, 0:XCH]
    sib_row.start()
    pl.when(far_left)(lambda: far_row.start())

    def lines(ref, spans):
        return [jnp.concatenate([ref[n:n + 1, span] for span in spans], axis=1) for n in range(3)]

    def queries(who):
        return [qd[who, n].reshape(QALL, DIM) for n in range(2)] + [row[who, n:n + 1, :] for n in range(3)]

    def own_rows(lo, hi):
        q, do = (qd[0, n, :, lo:hi].reshape(HEADS * (hi - lo), DIM) for n in range(2))
        return [q, do] + lines(row.at[0], [slice(g * ROWS + lo, g * ROWS + hi) for g in range(HEADS)])

    def part(query, kv, off, size, first_key, low=None, dq_rows=None, want_kv=True):
        q, do, lse, dot, start = query
        k = kv[0, off:off + size, :]
        v = kv[1, off:off + size, :]
        width = q.shape[0]
        key = lax.broadcasted_iota(jnp.int32, (size, width), 0)
        keep = (first_key + off + key).astype(F32) >= start
        if low is not None:
            keep = keep & (key <= lax.rem(lax.broadcasted_iota(jnp.int32, (size, width), 1), ROWS - low))
        s = lax.dot_general(k, q, NT, preferred_element_type=F32)
        dp = lax.dot_general(v, do, NT, preferred_element_type=F32)
        p = jnp.exp2(s * (scale * LOG2E) - lse)
        p = jnp.where(keep, p, 0.0)
        ds = (p * (dp - dot)).astype(BF16)
        if dq_rows is not None:
            lo, hi = dq_rows
            dq = lax.dot_general(k, ds, TN, preferred_element_type=F32)
            if low == 0:
                dqt[...] = dq
            elif hi - lo == ROWS:
                dqt[...] += dq
            else:
                for g in range(HEADS):
                    dqt[:, g * ROWS + lo:g * ROWS + hi] += dq[:, g * (hi - lo):(g + 1) * (hi - lo)]
        if want_kv:
            dv = jnp.dot(p.astype(BF16), do, preferred_element_type=F32)
            dk = jnp.dot(ds, q, preferred_element_type=F32)
            return dk, dv

    everything = (0, ROWS)

    for off in range(0, ROWS, XCH):
        dk, dv = part(own_rows(off, ROWS), kvown, off, XCH, rank * ROWS, low=off, dq_rows=(off, ROWS))
        own[0, off:off + XCH] = dk
        own[1, off:off + XCH] = dv

    pl.when(x_ret)(lambda: [kv_x(i).start() for i in range(NX)] and None)

    def lstep(n):
        off, size = STEPS[n]
        pieces = [(i, LOFF[i], LSIZE[i]) for i in range(NL) if off <= LOFF[i] < off + size]
        for piece in pieces:
            kv_right(*piece).wait_recv()
            kv_relay(*piece).start()
        mine_kv = kvl.at[core]
        dk, dv = part(queries(0), mine_kv, off, size, (rank - 2) * ROWS, dq_rows=everything)
        if n == 0:
            @pl.when(rank != 4)
            def _():
                sib_qd.wait_recv()
                sib_row.wait_recv()
        dk2, dv2 = part(queries(1), mine_kv, off, size, (rank - 2) * ROWS)
        mine[0, off:off + size] = dk + dk2
        mine[1, off:off + size] = dv + dv2

        @pl.when(rank != 4)
        def _():
            for piece in pieces:
                give_left(*piece).start()

        @pl.when(rank == 4)
        def _():
            for piece in pieces:
                (give_relay if piece[0] < NRLY else give_left)(*piece).start()

    def sib_keys(off):
        dk, dv = part(queries(1), kvown, off, XCH, rank * ROWS)
        own[0, off:off + XCH] += dk
        own[1, off:off + XCH] += dv

    @pl.when(rank == 4)
    def _():
        sib_qd.wait_recv()
        sib_row.wait_recv()
        sib_keys(0)

    @pl.when(chip == 3)
    def _():
        bounce().wait_recv()
        bounce_on().start()

    @pl.when(has_l)
    def _():
        for n in range(len(STEPS)):
            lstep(n)

    @pl.when(far_left)
    def _():
        kv_x(1).wait_recv()
        dk, dv = part(queries(0), kvx, XCH, XCH, x_from * ROWS, dq_rows=everything)
        xout[0] = dk
        xout[1] = dv
        give_x().start()
        kv_x(0).wait_recv()
        part(own_rows(0, XCH), kvx, 0, XCH, x_from * ROWS, dq_rows=(0, XCH), want_kv=False)

    @pl.when(has_l)
    def _():
        for off in range(0, ROWS, XCH):
            for i in range(NL):
                if off <= LOFF[i] < off + XCH:
                    kv_relayed(i, LOFF[i], LSIZE[i]).wait_recv()
            part(queries(0), kvl.at[1 - core], off, XCH, (sib - 2) * ROWS, dq_rows=everything, want_kv=False)

    @pl.when(chip == 0)
    def _():
        sib_qd.wait_recv()
        sib_row.wait_recv()

    @pl.when(core == 1)
    def _():
        for i in range(NX):
            kv_x(i).wait_recv()
            part(queries(0), kvx, i * XCH, XCH, x_from * ROWS, dq_rows=everything, want_kv=False)

    @pl.when(core == 0)
    def _():
        pl.when(rank != 4)(lambda: sib_keys(0))
        sib_keys(XCH)

    @pl.when(far_right)
    def _():
        far_qd.wait_recv()
        far_row.wait_recv()
        far = [qfar[n].reshape(HEADS * XCH, DIM) for n in range(2)] + [rfar[1, n:n + 1, :] for n in range(3)]
        dk, dv = part(far, kvown, 0, XCH, rank * ROWS)
        own[0, 0:XCH] += dk
        own[1, 0:XCH] += dv

    @pl.when(rank == 0)
    def _():
        for i in range(NRLY):
            give_relay(i, LOFF[i], LSIZE[i]).wait_recv()
            pass_on(i, LOFF[i], LSIZE[i]).start()

    for g in range(HEADS):
        lanes = slice(g * ROWS, (g + 1) * ROWS)
        dq_ref[lanes] = (dqt[:, lanes].T * scale).astype(BF16)

    for i in range(NL):
        span = slice(LOFF[i], LOFF[i] + LSIZE[i])

        @pl.when(has_r)
        def _():
            give_left(i, LOFF[i], LSIZE[i]).wait_recv()
            own[:, span] += lret[:, span]

        if i == NL - 1:
            @pl.when(far_right)
            def _():
                give_x().wait_recv()
                own[:, XCH:] += xret[...]
            span = slice(XCH, ROWS)
        elif LOFF[i] >= XCH:
            continue
        dk_ref[span, :] = (own[0, span] * scale).astype(BF16)
        dv_ref[span, :] = own[1, span].astype(BF16)

    for i in range(NL):
        at = (i, LOFF[i], LSIZE[i])
        pl.when(has_r)(lambda: kv_right(*at).wait_send())

        @pl.when(has_l)
        def _():
            kv_relay(*at).wait_send()
            give_left(*at).wait_send()

        if i < NRLY:
            pl.when(rank == 0)(lambda: pass_on(*at).wait_send())
    for i in range(NX):
        pl.when(x_ret)(lambda: kv_x(i).wait_send())
    sib_qd.wait_send()
    sib_row.wait_send()

    pl.when(chip == 3)(lambda: bounce_on().wait_send())

    @pl.when(far_left)
    def _():
        far_qd.wait_send()
        far_row.wait_send()
        give_x().wait_send()


def write_out(dq_ref, dk_ref, dv_ref, dq_hbm, dk_hbm, dv_hbm, sem):
    copies = [pltpu.make_async_copy(src, dst, sem.at[n]) for n, (src, dst) in enumerate([
        (dq_ref, dq_hbm), (dk_ref, dk_hbm), (dv_ref, dv_hbm)])]
    for copy in copies:
        copy.start()
    for copy in copies:
        copy.wait()


def solution(mesh):
    def local(queries, keys, values, attn_out, logsumexp, d_out, cu_seqlens):
        rows, heads, head = queries.shape
        flat = lambda a: jnp.transpose(a, (1, 0, 2))
        kv = pltpu.VMEM((2, rows, head), BF16)
        sums = pltpu.VMEM((2, rows, head), F32)
        row = pltpu.VMEM((2, 8, QALL), F32)
        qd = pltpu.VMEM((2, 2, heads, rows, head), BF16)
        xsum = pltpu.VMEM((2, XCH, head), F32)
        dma = pltpu.SemaphoreType.DMA
        anyspec = pl.BlockSpec(memory_space=pl.ANY)
        vspec = pl.BlockSpec(memory_space=pltpu.VMEM)
        dq, dk, dv = pl.pallas_call(
            kernel,
            out_shape=(pltpu.VMEM((QALL, head), BF16), pltpu.VMEM((rows, head), BF16), pltpu.VMEM((rows, head), BF16)),
            in_specs=[anyspec] * 7,
            out_specs=(vspec, vspec, vspec),
            scratch_shapes=[pltpu.SMEM((NBOUND,), jnp.int32), qd, row, pltpu.VMEM((2, heads, XCH, head), BF16),
                            pltpu.VMEM((2, 8, heads * XCH), F32), pltpu.VMEM((heads, rows, head), BF16),
                            pltpu.VMEM((heads, rows), F32), kv, kv, pltpu.VMEM((2, 2, rows, head), BF16),
                            pltpu.VMEM((2, LSIZE[-1], head), BF16),
                            pltpu.VMEM((head, QALL), F32), sums, sums, xsum, sums, xsum, sums,
                            dma((7,)), dma((4,)), dma((4,))] + [dma((NL,))] * 8 + [dma((NX,))] * 6,
            compiler_params=pltpu.CompilerParams(collective_id=0, has_side_effects=True,
                                                 vmem_limit_bytes=48 << 20),
        )(*[pltpu.with_memory_space_constraint(a, pltpu.HBM) for a in (
            cu_seqlens, flat(queries), keys, values, flat(attn_out), logsumexp.T, flat(d_out))])
        dq, dk, dv = pl.pallas_call(
            write_out,
            out_shape=(jax.ShapeDtypeStruct(dq.shape, BF16), jax.ShapeDtypeStruct(dk.shape, BF16),
                       jax.ShapeDtypeStruct(dv.shape, BF16)),
            in_specs=[vspec] * 3,
            out_specs=(anyspec,) * 3,
            scratch_shapes=[dma((3,))],
            compiler_params=pltpu.CompilerParams(vmem_limit_bytes=4 << 20),
        )(dq, dk, dv)
        return jnp.transpose(dq.reshape(heads, rows, head), (1, 0, 2)), dk, dv

    seq = P(("dp", "cpo", "cp"))
    return jax.shard_map(local, mesh=mesh, in_specs=(seq,) * 6 + (P("dp"),), out_specs=(seq, seq, seq), check_vma=False)
```

time: 28 us -> 23.7 us (0.85)
  the two profiles are of different devices: /device:TPU:1 before, /device:TPU:0 now
where the time goes in v3:
time: 23.7 us; the launch traced here: 23.6 us
  Pallas kernels  22.8 us (96%)
  between operations  0.8 us (3%)
    pallas_call x1, Pallas kernels, local(): pl.pallas_call(kernel, out_shape=(pltpu.VMEM((QALL, head), BF16), pltpu.V...  22 us
    pallas_call x1, Pallas kernels, local(): pl.pallas_call(write_out, out_shape=(jax.ShapeDtypeStruct(dq.shape, BF16)...  0.86 us

profile of v3, /device:TPU:0, one launch (start us, length us, event | category | flops | bytes accessed | tf_op | source)
XLA Modules:
  0.0 23.6 jit_solution(15123015594409443240)
XLA Ops:
  0.6 22.0 %shard_map.94 = (bf16[1536,128]{1,0:T(8,128)(2,1)S(1)}, bf16[512,128]{1,0:T(8,128)(2,1)S(1)}, bf16[512,128]{1,0:T(8,128)(2,1)S(1)}) custom-call(s32[14]{0:T(128)} %cu_hbm.1, bf16[3,512,128]{2,1,0:T(8,128)(2,1)} %bitcast.7, bf16[512,128]{1,0:T(8,128)(2,1)} %k_hbm.1, bf16[512,128]{1,0:T(8,128)(2,1)} %v_hbm.1, bf16[3,512,128]{2,1,0:T(8,128)(2,1)} %bitcast.8, ...), custom_call_target="tpu_custom_call" | custom-call | tf_op jit(solution)/shard_map/pallas_call | solution.py:374
  22.6 0.9 %shard_map.95 = (bf16[1536,128]{1,0:T(8,128)(2,1)}, bf16[512,128]{1,0:T(8,128)(2,1)}, bf16[512,128]{1,0:T(8,128)(2,1)}) custom-call(bf16[1536,128]{1,0:T(8,128)(2,1)S(1)} %get-tuple-element.9.dq_ref, bf16[512,128]{1,0:T(8,128)(2,1)S(1)} %get-tuple-element.10.dk_ref, bf16[512,128]{1,0:T(8,128)(2,1)S(1)} %get-tuple-element.11.dv_ref), custom_call_target="tpu_custom_call" | custom-call | tf_op jit(solution)/shard_map/pallas_call | solution.py:389

commit v4 on v3

--- a/solution.py
+++ b/solution.py
@@ -14,10 +14,11 @@
 QALL = HEADS * ROWS
 XCH = 256
 NX = ROWS // XCH
+PCH = 128
 LSIZE = (64, 64, 128, 128, 128)
 LOFF = (0, 64, 128, 256, 384)
 NL = len(LSIZE)
-NRLY = 4
+NRLY = 5
 STEPS = tuple(zip(LOFF, LSIZE))
 LOG2E = math.log2(math.e)
 MESH = pl.DeviceIdType.MESH
@@ -60,21 +61,23 @@
 
     far_right = (core == 1) & (chip <= 1)
     far_left = (core == 0) & (chip >= 2)
-    pl.when(has_l)(lambda: greet(rank - 2))
-    pl.when(has_r)(lambda: greet(rank + 2))
+    left = sib - 2
+    right = sib + 2
+    pl.when(has_l)(lambda: greet(left))
+    pl.when(has_r)(lambda: greet(right))
     pl.when(far_right)(lambda: greet(rank + 3))
     pl.when(far_left)(lambda: greet(rank - 3))
     pl.when(chip == 1)(lambda: greet(rank + 4))
     pl.when(chip == 3)(lambda: greet(rank - 4))
-    pl.when(rank == 0)(lambda: greet(4))
-    pl.when(rank == 4)(lambda: greet(0))
+    pl.when(rank == 1)(lambda: greet(5))
+    pl.when(rank == 5)(lambda: greet(1))
     greet(sib)
     for copy in loads[2:]:
         copy.start()
     one = jnp.int32(1)
     zero = jnp.int32(0)
     count = one
-    for there in (has_l, has_r, far_right, far_left, chip == 1, chip == 3, rank == 0, rank == 4):
+    for there in (has_l, has_r, far_right, far_left, chip == 1, chip == 3, rank == 1, rank == 5):
         count = count + jnp.where(there, one, zero)
     pl.semaphore_wait(barrier, count)
 
@@ -89,7 +92,10 @@
         return remote(src, dst, sb_s.at[n], sb_r.at[n], other)
 
     def kv_right(i, off, size):
-        return remote(kvown.at[:, rows(off, size)], kvl.at[core, :, rows(off, size)], kv_s.at[i], kv_r.at[i], rank + 2)
+        return remote(kvown.at[:, rows(off, size)], kvl.at[core, :, rows(off, size)], kv_s.at[i], kv_r.at[i], right)
+
+    def kv_in(i, off, size):
+        return remote(kvown.at[:, rows(off, size)], kvl.at[1 - core, :, rows(off, size)], kv_s.at[i], kv_r.at[i], left)
 
     last = pl.ds(LOFF[-1], LSIZE[-1])
 
@@ -97,26 +103,27 @@
         return remote(kvown.at[:, last], kvb, kv_s.at[NL - 1], bn_r.at[0], rank + 4)
 
     def bounce_on():
-        return remote(kvb, kvl.at[core, :, last], bn_s.at[0], kv_r.at[NL - 1], rank - 2)
+        return remote(kvb, kvl.at[core, :, last], bn_s.at[0], kv_r.at[NL - 1], left)
 
     def kv_relay(i, off, size):
-        return remote(kvl.at[core, :, rows(off, size)], kvl.at[core, :, rows(off, size)], re_s.at[i], re_r.at[i], sib)
-
-    def kv_relayed(i, off, size):
         part = kvl.at[1 - core, :, rows(off, size)]
         return remote(part, part, re_s.at[i], re_r.at[i], sib)
 
+    def kv_relayed(i, off, size):
+        part = kvl.at[core, :, rows(off, size)]
+        return remote(part, part, re_s.at[i], re_r.at[i], sib)
+
     def kv_x(i):
         return remote(kvown.at[:, rows(i * XCH, XCH)], kvx.at[:, rows(i * XCH, XCH)], kx_s.at[i], kx_r.at[i], x_to)
 
-    def give_x():
-        return remote(xout, xret, xo_s.at[0], xo_r.at[0], rank - 3)
+    def give_x(j):
+        return remote(xout.at[:, rows(j * PCH, PCH)], xret.at[:, rows(j * PCH, PCH)], xo_s.at[j], xo_r.at[j], rank - 3)
 
     def give_left(i, off, size):
-        return remote(mine.at[:, rows(off, size)], lret.at[:, rows(off, size)], le_s.at[i], le_r.at[i], rank - 2)
+        return remote(mine.at[:, rows(off, size)], lret.at[:, rows(off, size)], le_s.at[i], le_r.at[i], left)
 
     def give_relay(i, off, size):
-        return remote(mine.at[:, rows(off, size)], rly.at[:, rows(off, size)], le_s.at[i], ry_r.at[i], 0)
+        return remote(mine.at[:, rows(off, size)], rly.at[:, rows(off, size)], le_s.at[i], ry_r.at[i], 1)
 
     def pass_on(i, off, size):
         return remote(rly.at[:, rows(off, size)], lret.at[:, rows(off, size)], ry_s.at[i], le_r.at[i], 2)
@@ -209,25 +216,25 @@
         off, size = STEPS[n]
         pieces = [(i, LOFF[i], LSIZE[i]) for i in range(NL) if off <= LOFF[i] < off + size]
         for piece in pieces:
-            kv_right(*piece).wait_recv()
+            kv_in(*piece).wait_recv()
             kv_relay(*piece).start()
-        mine_kv = kvl.at[core]
-        dk, dv = part(queries(0), mine_kv, off, size, (rank - 2) * ROWS, dq_rows=everything)
+        mine_kv = kvl.at[1 - core]
+        dk, dv = part(queries(0), mine_kv, off, size, left * ROWS, dq_rows=everything)
         if n == 0:
             @pl.when(rank != 4)
             def _():
                 sib_qd.wait_recv()
                 sib_row.wait_recv()
-        dk2, dv2 = part(queries(1), mine_kv, off, size, (rank - 2) * ROWS)
+        dk2, dv2 = part(queries(1), mine_kv, off, size, left * ROWS)
         mine[0, off:off + size] = dk + dk2
         mine[1, off:off + size] = dv + dv2
 
-        @pl.when(rank != 4)
+        @pl.when(rank != 5)
         def _():
             for piece in pieces:
                 give_left(*piece).start()
 
-        @pl.when(rank == 4)
+        @pl.when(rank == 5)
         def _():
             for piece in pieces:
                 (give_relay if piece[0] < NRLY else give_left)(*piece).start()
@@ -259,7 +266,8 @@
         dk, dv = part(queries(0), kvx, XCH, XCH, x_from * ROWS, dq_rows=everything)
         xout[0] = dk
         xout[1] = dv
-        give_x().start()
+        give_x(0).start()
+        give_x(1).start()
         kv_x(0).wait_recv()
         part(own_rows(0, XCH), kvx, 0, XCH, x_from * ROWS, dq_rows=(0, XCH), want_kv=False)
 
@@ -269,7 +277,7 @@
             for i in range(NL):
                 if off <= LOFF[i] < off + XCH:
                     kv_relayed(i, LOFF[i], LSIZE[i]).wait_recv()
-            part(queries(0), kvl.at[1 - core], off, XCH, (sib - 2) * ROWS, dq_rows=everything, want_kv=False)
+            part(queries(0), kvl.at[core], off, XCH, (rank - 2) * ROWS, dq_rows=everything, want_kv=False)
 
     @pl.when(chip == 0)
     def _():
@@ -296,7 +304,7 @@
         own[0, 0:XCH] += dk
         own[1, 0:XCH] += dv
 
-    @pl.when(rank == 0)
+    @pl.when(rank == 1)
     def _():
         for i in range(NRLY):
             give_relay(i, LOFF[i], LSIZE[i]).wait_recv()
@@ -305,6 +313,31 @@
     for g in range(HEADS):
         lanes = slice(g * ROWS, (g + 1) * ROWS)
         dq_ref[lanes] = (dqt[:, lanes].T * scale).astype(BF16)
+
+    for i in range(NL):
+        at = (i, LOFF[i], LSIZE[i])
+        pl.when(has_r)(lambda: kv_right(*at).wait_send())
+
+        @pl.when(has_l)
+        def _():
+            kv_relay(*at).wait_send()
+            give_left(*at).wait_send()
+
+        if i < NRLY:
+            pl.when(rank == 1)(lambda: pass_on(*at).wait_send())
+    for i in range(NX):
+        pl.when(x_ret)(lambda: kv_x(i).wait_send())
+    sib_qd.wait_send()
+    sib_row.wait_send()
+
+    pl.when(chip == 3)(lambda: bounce_on().wait_send())
+
+    @pl.when(far_left)
+    def _():
+        far_qd.wait_send()
+        far_row.wait_send()
+        give_x(0).wait_send()
+        give_x(1).wait_send()
 
     for i in range(NL):
         span = slice(LOFF[i], LOFF[i] + LSIZE[i])
@@ -314,40 +347,14 @@
             give_left(i, LOFF[i], LSIZE[i]).wait_recv()
             own[:, span] += lret[:, span]
 
-        if i == NL - 1:
+        if LOFF[i] >= XCH:
             @pl.when(far_right)
             def _():
-                give_x().wait_recv()
-                own[:, XCH:] += xret[...]
-            span = slice(XCH, ROWS)
-        elif LOFF[i] >= XCH:
-            continue
+                give_x(i - NL + 2).wait_recv()
+                own[:, span] += xret[:, LOFF[i] - XCH:LOFF[i] - XCH + LSIZE[i]]
+
         dk_ref[span, :] = (own[0, span] * scale).astype(BF16)
         dv_ref[span, :] = own[1, span].astype(BF16)
-
-    for i in range(NL):
-        at = (i, LOFF[i], LSIZE[i])
-        pl.when(has_r)(lambda: kv_right(*at).wait_send())
-
-        @pl.when(has_l)
-        def _():
-            kv_relay(*at).wait_send()
-            give_left(*at).wait_send()
-
-        if i < NRLY:
-            pl.when(rank == 0)(lambda: pass_on(*at).wait_send())
-    for i in range(NX):
-        pl.when(x_ret)(lambda: kv_x(i).wait_send())
-    sib_qd.wait_send()
-    sib_row.wait_send()
-
-    pl.when(chip == 3)(lambda: bounce_on().wait_send())
-
-    @pl.when(far_left)
-    def _():
-        far_qd.wait_send()
-        far_row.wait_send()
-        give_x().wait_send()
 
 
 def write_out(dq_ref, dk_ref, dv_ref, dq_hbm, dk_hbm, dv_hbm, sem):

time: 23.7 us -> 23.1 us (0.975)
  Pallas kernels: 22.8 us -> 22.2 us
    pallas_call x1, Pallas kernels: 22 us -> 21.4 us  [local(): pl.pallas_call(kernel, out_shape=(pltpu.VMEM((QALL, head), BF16), pltpu.V...]
where the time goes in v4:
time: 23.1 us; the launch traced here: 23 us
  Pallas kernels  22.2 us (96%)
  between operations  0.8 us (3%)
    pallas_call x1, Pallas kernels, local(): pl.pallas_call(kernel, out_shape=(pltpu.VMEM((QALL, head), BF16), pltpu.V...  21.4 us
    pallas_call x1, Pallas kernels, local(): pl.pallas_call(write_out, out_shape=(jax.ShapeDtypeStruct(dq.shape, BF16)...  0.86 us

profile of v4, /device:TPU:0, one launch (start us, length us, event | category | flops | bytes accessed | tf_op | source)
XLA Modules:
  0.0 23.0 jit_solution(1972782266590894837)
XLA Ops:
  0.6 21.4 %shard_map.94 = (bf16[1536,128]{1,0:T(8,128)(2,1)S(1)}, bf16[512,128]{1,0:T(8,128)(2,1)S(1)}, bf16[512,128]{1,0:T(8,128)(2,1)S(1)}) custom-call(s32[14]{0:T(128)} %cu_hbm.1, bf16[3,512,128]{2,1,0:T(8,128)(2,1)} %bitcast.7, bf16[512,128]{1,0:T(8,128)(2,1)} %k_hbm.1, bf16[512,128]{1,0:T(8,128)(2,1)} %v_hbm.1, bf16[3,512,128]{2,1,0:T(8,128)(2,1)} %bitcast.8, ...), custom_call_target="tpu_custom_call" | custom-call | tf_op jit(solution)/shard_map/pallas_call | solution.py:381
  22.0 0.9 %shard_map.95 = (bf16[1536,128]{1,0:T(8,128)(2,1)}, bf16[512,128]{1,0:T(8,128)(2,1)}, bf16[512,128]{1,0:T(8,128)(2,1)}) custom-call(bf16[1536,128]{1,0:T(8,128)(2,1)S(1)} %get-tuple-element.9.dq_ref, bf16[512,128]{1,0:T(8,128)(2,1)S(1)} %get-tuple-element.10.dk_ref, bf16[512,128]{1,0:T(8,128)(2,1)S(1)} %get-tuple-element.11.dv_ref), custom_call_target="tpu_custom_call" | custom-call | tf_op jit(solution)/shard_map/pallas_call | solution.py:396

commit v5 on v4

--- a/solution.py
+++ b/solution.py
@@ -34,16 +34,19 @@
 
 def kernel(cu_hbm, q_hbm, k_hbm, v_hbm, o_hbm, lse_hbm, do_hbm, dq_ref, dk_ref, dv_ref,
            cu_ref, qd, row, qfar, rfar, o_ref, lse_ref, kvown, kvx, kvl, kvb, dqt, own, mine, xout, lret, xret, rly,
-           in_sem, sb_s, sb_r, kv_s, kv_r, re_s, re_r, le_s, le_r, ry_s, ry_r, kx_s, kx_r, xo_s, xo_r, bn_s, bn_r):
+           in_sem, out_sem, lend_r, kv_r, re_r, le_r, kx_r, xo_r):
     rank = lax.axis_index("cpo") * 4 + lax.axis_index("cp")
     core = rank & 1
     chip = rank >> 1
     sib = rank + 1 - 2 * core
     scale = DIM ** -0.5
 
-    loads = [pltpu.make_async_copy(src, dst, in_sem.at[n]) for n, (src, dst) in enumerate([
+    sems = (0, 0, 1, 1, 2, 3, 4)
+    loads = [pltpu.make_async_copy(src, dst, in_sem.at[n]) for n, (src, dst) in zip(sems, [
         (k_hbm, kvown.at[0]), (v_hbm, kvown.at[1]), (do_hbm, qd.at[0, 1]), (q_hbm, qd.at[0, 0]), (o_hbm, o_ref),
         (lse_hbm, lse_ref), (cu_hbm, cu_ref)])]
+    kv_loaded = pltpu.make_async_copy(kvown, kvown, in_sem.at[0])
+    qd_loaded = pltpu.make_async_copy(qd.at[0], qd.at[0], in_sem.at[1])
     loads[0].start()
     loads[1].start()
 
@@ -88,48 +91,56 @@
     def rows(off, size):
         return pl.ds(off, size)
 
-    def lend(src, dst, n, other):
-        return remote(src, dst, sb_s.at[n], sb_r.at[n], other)
+    kv_s, kx_s, re_s, le_s, xo_s = in_sem.at[0], out_sem.at[0], out_sem.at[1], out_sem.at[2], out_sem.at[3]
+    last = pl.ds(LOFF[-1], LSIZE[-1])
+    whole = (NL, 0, ROWS)
+    halves = ((0, 0, XCH), (NL - 1, XCH, XCH))
+
+    def half_of(i):
+        return min(i // 3, 1)
+
+    def third(i):
+        return min(max(i - 2, 0), 2)
+
+    def lend(src, dst, s_n, r_n, other):
+        return remote(src, dst, in_sem.at[s_n], lend_r.at[r_n], other)
 
     def kv_right(i, off, size):
-        return remote(kvown.at[:, rows(off, size)], kvl.at[core, :, rows(off, size)], kv_s.at[i], kv_r.at[i], right)
+        return remote(kvown.at[:, rows(off, size)], kvl.at[core, :, rows(off, size)], kv_s, kv_r.at[min(i, NL - 1)], right)
 
     def kv_in(i, off, size):
-        return remote(kvown.at[:, rows(off, size)], kvl.at[1 - core, :, rows(off, size)], kv_s.at[i], kv_r.at[i], left)
-
-    last = pl.ds(LOFF[-1], LSIZE[-1])
+        return remote(kvown.at[:, rows(off, size)], kvl.at[1 - core, :, rows(off, size)], kv_s, kv_r.at[i], left)
 
     def bounce():
-        return remote(kvown.at[:, last], kvb, kv_s.at[NL - 1], bn_r.at[0], rank + 4)
+        return remote(kvown.at[:, last], kvb, kv_s, le_r.at[0], rank + 4)
 
     def bounce_on():
-        return remote(kvb, kvl.at[core, :, last], bn_s.at[0], kv_r.at[NL - 1], left)
+        return remote(kvb, kvl.at[core, :, last], kv_s, kv_r.at[NL - 1], left)
 
     def kv_relay(i, off, size):
         part = kvl.at[1 - core, :, rows(off, size)]
-        return remote(part, part, re_s.at[i], re_r.at[i], sib)
+        return remote(part, part, re_s, re_r.at[half_of(i)], sib)
 
     def kv_relayed(i, off, size):
         part = kvl.at[core, :, rows(off, size)]
-        return remote(part, part, re_s.at[i], re_r.at[i], sib)
-
-    def kv_x(i):
-        return remote(kvown.at[:, rows(i * XCH, XCH)], kvx.at[:, rows(i * XCH, XCH)], kx_s.at[i], kx_r.at[i], x_to)
-
-    def give_x(j):
-        return remote(xout.at[:, rows(j * PCH, PCH)], xret.at[:, rows(j * PCH, PCH)], xo_s.at[j], xo_r.at[j], rank - 3)
+        return remote(part, part, re_s, re_r.at[half_of(i)], sib)
+
+    def kv_x():
+        return remote(kvown, kvx, kx_s, kx_r.at[0], x_to)
+
+    def give_x():
+        return remote(xout, xret, xo_s, xo_r.at[0], rank - 3)
 
     def give_left(i, off, size):
-        return remote(mine.at[:, rows(off, size)], lret.at[:, rows(off, size)], le_s.at[i], le_r.at[i], left)
+        return remote(mine.at[:, rows(off, size)], lret.at[:, rows(off, size)], le_s, le_r.at[third(i)], left)
 
     def give_relay(i, off, size):
-        return remote(mine.at[:, rows(off, size)], rly.at[:, rows(off, size)], le_s.at[i], ry_r.at[i], 1)
+        return remote(mine.at[:, rows(off, size)], rly.at[:, rows(off, size)], le_s, kv_r.at[i], 1)
 
     def pass_on(i, off, size):
-        return remote(rly.at[:, rows(off, size)], lret.at[:, rows(off, size)], ry_s.at[i], le_r.at[i], 2)
-
-    loads[0].wait()
-    loads[1].wait()
+        return remote(rly.at[:, rows(off, size)], lret.at[:, rows(off, size)], le_s, le_r.at[third(i)], 2)
+
+    kv_loaded.wait()
 
     @pl.when(has_r)
     def _():
@@ -138,17 +149,16 @@
             kv_right(i, LOFF[i], LSIZE[i]).start()
         pl.when(chip != 1)(lambda: kv_right(NL - 1, LOFF[-1], LSIZE[-1]).start())
 
-    loads[2].wait()
-    loads[3].wait()
-    sib_qd, sib_row = lend(qd.at[0], qd.at[1], 0, sib), lend(row.at[0], row.at[1], 1, sib)
+    qd_loaded.wait()
     far_to = jnp.where(core == 0, rank - 3, rank + 3)
-    far_qd, far_row = lend(qd.at[0, :, :, 0:XCH], qfar, 2, far_to), lend(rfar.at[0], rfar.at[1], 3, far_to)
+    sib_qd, sib_row = lend(qd.at[0], qd.at[1], 1, 0, sib), lend(row.at[0], row.at[1], 3, 1, sib)
+    far_qd, far_row = lend(qd.at[0, :, :, 0:XCH], qfar, 4, 2, far_to), lend(rfar.at[0], rfar.at[1], 2, 3, far_to)
+    loads[6].wait()
+    pl.when(far_left)(lambda: far_qd.start())
     sib_qd.start()
-    pl.when(far_left)(lambda: far_qd.start())
 
     pos = rank * ROWS + lax.broadcasted_iota(jnp.int32, (1, ROWS), 1)
     start = jnp.zeros((1, ROWS), jnp.int32)
-    loads[6].wait()
     for n in range(NBOUND):
         bound = cu_ref[n]
         start = jnp.where(bound <= pos, bound, start)
@@ -210,7 +220,7 @@
         own[0, off:off + XCH] = dk
         own[1, off:off + XCH] = dv
 
-    pl.when(x_ret)(lambda: [kv_x(i).start() for i in range(NX)] and None)
+    pl.when(x_ret)(lambda: kv_x().start())
 
     def lstep(n):
         off, size = STEPS[n]
@@ -262,21 +272,17 @@
 
     @pl.when(far_left)
     def _():
-        kv_x(1).wait_recv()
+        kv_x().wait_recv()
         dk, dv = part(queries(0), kvx, XCH, XCH, x_from * ROWS, dq_rows=everything)
         xout[0] = dk
         xout[1] = dv
-        give_x(0).start()
-        give_x(1).start()
-        kv_x(0).wait_recv()
+        give_x().start()
         part(own_rows(0, XCH), kvx, 0, XCH, x_from * ROWS, dq_rows=(0, XCH), want_kv=False)
 
     @pl.when(has_l)
     def _():
         for off in range(0, ROWS, XCH):
-            for i in range(NL):
-                if off <= LOFF[i] < off + XCH:
-                    kv_relayed(i, LOFF[i], LSIZE[i]).wait_recv()
+            kv_relayed(*halves[off // XCH]).wait_recv()
             part(queries(0), kvl.at[core], off, XCH, (rank - 2) * ROWS, dq_rows=everything, want_kv=False)
 
     @pl.when(chip == 0)
@@ -286,8 +292,8 @@
 
     @pl.when(core == 1)
     def _():
+        kv_x().wait_recv()
         for i in range(NX):
-            kv_x(i).wait_recv()
             part(queries(0), kvx, i * XCH, XCH, x_from * ROWS, dq_rows=everything, want_kv=False)
 
     @pl.when(core == 0)
@@ -314,44 +320,38 @@
         lanes = slice(g * ROWS, (g + 1) * ROWS)
         dq_ref[lanes] = (dqt[:, lanes].T * scale).astype(BF16)
 
-    for i in range(NL):
-        at = (i, LOFF[i], LSIZE[i])
-        pl.when(has_r)(lambda: kv_right(*at).wait_send())
-
-        @pl.when(has_l)
-        def _():
-            kv_relay(*at).wait_send()
-            give_left(*at).wait_send()
-
-        if i < NRLY:
-            pl.when(rank == 1)(lambda: pass_on(*at).wait_send())
-    for i in range(NX):
-        pl.when(x_ret)(lambda: kv_x(i).wait_send())
+    pl.when(has_r)(lambda: kv_right(*whole).wait_send())
+    pl.when(chip == 3)(lambda: bounce_on().wait_send())
+    pl.when(x_ret)(lambda: kv_x().wait_send())
     sib_qd.wait_send()
     sib_row.wait_send()
 
-    pl.when(chip == 3)(lambda: bounce_on().wait_send())
-
     @pl.when(far_left)
     def _():
         far_qd.wait_send()
         far_row.wait_send()
-        give_x(0).wait_send()
-        give_x(1).wait_send()
-
-    for i in range(NL):
-        span = slice(LOFF[i], LOFF[i] + LSIZE[i])
+        give_x().wait_send()
+
+    @pl.when(has_l)
+    def _():
+        kv_relay(*whole).wait_send()
+        give_left(*whole).wait_send()
+
+    pl.when(rank == 1)(lambda: pass_on(*whole).wait_send())
+
+    for i, off, size in ((0, 0, XCH), (3, LOFF[3], LSIZE[3]), (4, LOFF[4], LSIZE[4])):
+        span = slice(off, off + size)
 
         @pl.when(has_r)
         def _():
-            give_left(i, LOFF[i], LSIZE[i]).wait_recv()
+            give_left(i, off, size).wait_recv()
             own[:, span] += lret[:, span]
 
-        if LOFF[i] >= XCH:
+        if off == XCH:
             @pl.when(far_right)
             def _():
-                give_x(i - NL + 2).wait_recv()
-                own[:, span] += xret[:, LOFF[i] - XCH:LOFF[i] - XCH + LSIZE[i]]
+                give_x().wait_recv()
+                own[:, XCH:] += xret[...]
 
         dk_ref[span, :] = (own[0, span] * scale).astype(BF16)
         dv_ref[span, :] = own[1, span].astype(BF16)
@@ -388,7 +388,7 @@
                             pltpu.VMEM((heads, rows), F32), kv, kv, pltpu.VMEM((2, 2, rows, head), BF16),
                             pltpu.VMEM((2, LSIZE[-1], head), BF16),
                             pltpu.VMEM((head, QALL), F32), sums, sums, xsum, sums, xsum, sums,
-                            dma((7,)), dma((4,)), dma((4,))] + [dma((NL,))] * 8 + [dma((NX,))] * 6,
+                            dma((5,)), dma((4,)), dma((4,)), dma((NL,)), dma((2,)), dma((3,)), dma((1,)), dma((1,))],
             compiler_params=pltpu.CompilerParams(collective_id=0, has_side_effects=True,
                                                  vmem_limit_bytes=48 << 20),
         )(*[pltpu.with_memory_space_constraint(a, pltpu.HBM) for a in (

time: 23.1 us -> 22.7 us (0.983)
  Pallas kernels: 22.2 us -> 21.8 us
    pallas_call x1, Pallas kernels: 21.4 us -> 21 us  [local(): pl.pallas_call(kernel, out_shape=(pltpu.VMEM((QALL, head), BF16), pltpu.V...]
where the time goes in v5:
time: 22.7 us; the launch traced here: 22.6 us
  Pallas kernels  21.8 us (96%)
  between operations  0.8 us (4%)
    pallas_call x1, Pallas kernels, local(): pl.pallas_call(kernel, out_shape=(pltpu.VMEM((QALL, head), BF16), pltpu.V...  21 us
    pallas_call x1, Pallas kernels, local(): pl.pallas_call(write_out, out_shape=(jax.ShapeDtypeStruct(dq.shape, BF16)...  0.86 us

profile of v5, /device:TPU:0, one launch (start us, length us, event | category | flops | bytes accessed | tf_op | source)
XLA Modules:
  0.0 22.6 jit_solution(13259496902258032664)
XLA Ops:
  0.6 21.0 %shard_map.94 = (bf16[1536,128]{1,0:T(8,128)(2,1)S(1)}, bf16[512,128]{1,0:T(8,128)(2,1)S(1)}, bf16[512,128]{1,0:T(8,128)(2,1)S(1)}) custom-call(s32[14]{0:T(128)} %cu_hbm.1, bf16[3,512,128]{2,1,0:T(8,128)(2,1)} %bitcast.7, bf16[512,128]{1,0:T(8,128)(2,1)} %k_hbm.1, bf16[512,128]{1,0:T(8,128)(2,1)} %v_hbm.1, bf16[3,512,128]{2,1,0:T(8,128)(2,1)} %bitcast.8, ...), custom_call_target="tpu_custom_call" | custom-call | tf_op jit(solution)/shard_map/pallas_call | solution.py:381
  21.6 0.9 %shard_map.95 = (bf16[1536,128]{1,0:T(8,128)(2,1)}, bf16[512,128]{1,0:T(8,128)(2,1)}, bf16[512,128]{1,0:T(8,128)(2,1)}) custom-call(bf16[1536,128]{1,0:T(8,128)(2,1)S(1)} %get-tuple-element.9.dq_ref, bf16[512,128]{1,0:T(8,128)(2,1)S(1)} %get-tuple-element.10.dk_ref, bf16[512,128]{1,0:T(8,128)(2,1)S(1)} %get-tuple-element.11.dv_ref), custom_call_target="tpu_custom_call" | custom-call | tf_op jit(solution)/shard_map/pallas_call | solution.py:396

commit v6 on v5

--- a/solution.py
+++ b/solution.py
@@ -15,11 +15,12 @@
 XCH = 256
 NX = ROWS // XCH
 PCH = 128
-LSIZE = (64, 64, 128, 128, 128)
-LOFF = (0, 64, 128, 256, 384)
+LSIZE = (64, 64, 128, 96, 160)
+LOFF = (0, 64, 128, 256, 352)
 NL = len(LSIZE)
-NRLY = 5
+NRLY = 4
 STEPS = tuple(zip(LOFF, LSIZE))
+RLYROWS = sum(LSIZE[:NRLY])
 LOG2E = math.log2(math.e)
 MESH = pl.DeviceIdType.MESH
 F32 = jnp.float32
@@ -222,12 +223,15 @@
 
     pl.when(x_ret)(lambda: kv_x().start())
 
-    def lstep(n):
+    def fetch(n):
+        kv_in(n, *STEPS[n]).wait_recv()
+        kv_relay(n, *STEPS[n]).start()
+
+    def lstep(n, fetched=False):
         off, size = STEPS[n]
-        pieces = [(i, LOFF[i], LSIZE[i]) for i in range(NL) if off <= LOFF[i] < off + size]
-        for piece in pieces:
-            kv_in(*piece).wait_recv()
-            kv_relay(*piece).start()
+        pieces = [(n, off, size)]
+        if not fetched:
+            fetch(n)
         mine_kv = kvl.at[1 - core]
         dk, dv = part(queries(0), mine_kv, off, size, left * ROWS, dq_rows=everything)
         if n == 0:
@@ -244,10 +248,10 @@
             for piece in pieces:
                 give_left(*piece).start()
 
-        @pl.when(rank == 5)
-        def _():
-            for piece in pieces:
-                (give_relay if piece[0] < NRLY else give_left)(*piece).start()
+        if n < NRLY:
+            pl.when(rank == 5)(lambda: give_relay(*pieces[0]).start())
+        else:
+            pl.when(rank == 5)(lambda: give_left(*pieces[0]).start())
 
     def sib_keys(off):
         dk, dv = part(queries(1), kvown, off, XCH, rank * ROWS)
@@ -267,8 +271,14 @@
 
     @pl.when(has_l)
     def _():
-        for n in range(len(STEPS)):
+        for n in range(NL - 2):
             lstep(n)
+        pl.when(rank != 2)(lambda: lstep(NL - 2))
+
+        @pl.when(rank == 2)
+        def _():
+            fetch(NL - 2)
+            fetch(NL - 1)
 
     @pl.when(far_left)
     def _():
@@ -277,6 +287,11 @@
         xout[0] = dk
         xout[1] = dv
         give_x().start()
+
+    pl.when(has_l & (rank != 2))(lambda: lstep(NL - 1))
+
+    @pl.when(far_left)
+    def _():
         part(own_rows(0, XCH), kvx, 0, XCH, x_from * ROWS, dq_rows=(0, XCH), want_kv=False)
 
     @pl.when(has_l)
@@ -299,6 +314,12 @@
     @pl.when(core == 0)
     def _():
         pl.when(rank != 4)(lambda: sib_keys(0))
+
+        @pl.when(rank == 2)
+        def _():
+            lstep(NL - 2, fetched=True)
+            lstep(NL - 1, fetched=True)
+
         sib_keys(XCH)
 
     @pl.when(far_right)
@@ -337,15 +358,10 @@
         kv_relay(*whole).wait_send()
         give_left(*whole).wait_send()
 
-    pl.when(rank == 1)(lambda: pass_on(*whole).wait_send())
+    pl.when(rank == 1)(lambda: pass_on(NL, 0, RLYROWS).wait_send())
 
     for i, off, size in ((0, 0, XCH), (3, LOFF[3], LSIZE[3]), (4, LOFF[4], LSIZE[4])):
         span = slice(off, off + size)
-
-        @pl.when(has_r)
-        def _():
-            give_left(i, off, size).wait_recv()
-            own[:, span] += lret[:, span]
 
         if off == XCH:
             @pl.when(far_right)
@@ -353,8 +369,16 @@
                 give_x().wait_recv()
                 own[:, XCH:] += xret[...]
 
-        dk_ref[span, :] = (own[0, span] * scale).astype(BF16)
-        dv_ref[span, :] = own[1, span].astype(BF16)
+        @pl.when(has_r)
+        def _():
+            give_left(i, off, size).wait_recv()
+            dk_ref[span, :] = ((own[0, span] + lret[0, span]) * scale).astype(BF16)
+            dv_ref[span, :] = (own[1, span] + lret[1, span]).astype(BF16)
+
+        @pl.when(chip == 3)
+        def _():
+            dk_ref[span, :] = (own[0, span] * scale).astype(BF16)
+            dv_ref[span, :] = own[1, span].astype(BF16)
 
 
 def write_out(dq_ref, dk_ref, dv_ref, dq_hbm, dk_hbm, dv_hbm, sem):

time: 22.7 us -> 22.1 us (0.974)
  the two profiles are of different devices: /device:TPU:0 before, /device:TPU:3 now
where the time goes in v6:
time: 22.1 us; the launch traced here: 22 us
  Pallas kernels  21.2 us (96%)
  between operations  0.8 us (4%)
    pallas_call x1, Pallas kernels, local(): pl.pallas_call(kernel, out_shape=(pltpu.VMEM((QALL, head), BF16), pltpu.V...  20.4 us
    pallas_call x1, Pallas kernels, local(): pl.pallas_call(write_out, out_shape=(jax.ShapeDtypeStruct(dq.shape, BF16)...  0.86 us

profile of v6, /device:TPU:3, one launch (start us, length us, event | category | flops | bytes accessed | tf_op | source)
XLA Modules:
  0.0 22.0 jit_solution(790119582800459393)
XLA Ops:
  0.6 20.4 %shard_map.94 = (bf16[1536,128]{1,0:T(8,128)(2,1)S(1)}, bf16[512,128]{1,0:T(8,128)(2,1)S(1)}, bf16[512,128]{1,0:T(8,128)(2,1)S(1)}) custom-call(s32[14]{0:T(128)} %cu_hbm.1, bf16[3,512,128]{2,1,0:T(8,128)(2,1)} %bitcast.7, bf16[512,128]{1,0:T(8,128)(2,1)} %k_hbm.1, bf16[512,128]{1,0:T(8,128)(2,1)} %v_hbm.1, bf16[3,512,128]{2,1,0:T(8,128)(2,1)} %bitcast.8, ...), custom_call_target="tpu_custom_call" | custom-call | tf_op jit(solution)/shard_map/pallas_call | solution.py:405
  21.0 0.9 %shard_map.95 = (bf16[1536,128]{1,0:T(8,128)(2,1)}, bf16[512,128]{1,0:T(8,128)(2,1)}, bf16[512,128]{1,0:T(8,128)(2,1)}) custom-call(bf16[1536,128]{1,0:T(8,128)(2,1)S(1)} %get-tuple-element.9.dq_ref, bf16[512,128]{1,0:T(8,128)(2,1)S(1)} %get-tuple-element.10.dk_ref, bf16[512,128]{1,0:T(8,128)(2,1)S(1)} %get-tuple-element.11.dv_ref), custom_call_target="tpu_custom_call" | custom-call | tf_op jit(solution)/shard_map/pallas_call | solution.py:420

commit v7 on v6

--- a/solution.py
+++ b/solution.py
@@ -250,8 +250,6 @@
 
         if n < NRLY:
             pl.when(rank == 5)(lambda: give_relay(*pieces[0]).start())
-        else:
-            pl.when(rank == 5)(lambda: give_left(*pieces[0]).start())
 
     def sib_keys(off):
         dk, dv = part(queries(1), kvown, off, XCH, rank * ROWS)
@@ -299,6 +297,7 @@
         for off in range(0, ROWS, XCH):
             kv_relayed(*halves[off // XCH]).wait_recv()
             part(queries(0), kvl.at[core], off, XCH, (rank - 2) * ROWS, dq_rows=everything, want_kv=False)
+        pl.when(rank == 5)(lambda: give_left(NL - 1, *STEPS[-1]).start())
 
     @pl.when(chip == 0)
     def _():

time: 22.1 us -> 22.1 us (level)
  no operation moved by 1% of the time
where the time goes in v7:
time: 22.1 us; the launch traced here: 22 us
  Pallas kernels  21.2 us (96%)
  between operations  0.8 us (4%)
    pallas_call x1, Pallas kernels, local(): pl.pallas_call(kernel, out_shape=(pltpu.VMEM((QALL, head), BF16), pltpu.V...  20.3 us
    pallas_call x1, Pallas kernels, local(): pl.pallas_call(write_out, out_shape=(jax.ShapeDtypeStruct(dq.shape, BF16)...  0.86 us

profile of v7, /device:TPU:3, one launch (start us, length us, event | category | flops | bytes accessed | tf_op | source)
XLA Modules:
  0.0 22.0 jit_solution(11935167495282111165)
XLA Ops:
  0.6 20.3 %shard_map.94 = (bf16[1536,128]{1,0:T(8,128)(2,1)S(1)}, bf16[512,128]{1,0:T(8,128)(2,1)S(1)}, bf16[512,128]{1,0:T(8,128)(2,1)S(1)}) custom-call(s32[14]{0:T(128)} %cu_hbm.1, bf16[3,512,128]{2,1,0:T(8,128)(2,1)} %bitcast.7, bf16[512,128]{1,0:T(8,128)(2,1)} %k_hbm.1, bf16[512,128]{1,0:T(8,128)(2,1)} %v_hbm.1, bf16[3,512,128]{2,1,0:T(8,128)(2,1)} %bitcast.8, ...), custom_call_target="tpu_custom_call" | custom-call | tf_op jit(solution)/shard_map/pallas_call | solution.py:404
  21.0 0.9 %shard_map.95 = (bf16[1536,128]{1,0:T(8,128)(2,1)}, bf16[512,128]{1,0:T(8,128)(2,1)}, bf16[512,128]{1,0:T(8,128)(2,1)}) custom-call(bf16[1536,128]{1,0:T(8,128)(2,1)S(1)} %get-tuple-element.9.dq_ref, bf16[512,128]{1,0:T(8,128)(2,1)S(1)} %get-tuple-element.10.dk_ref, bf16[512,128]{1,0:T(8,128)(2,1)S(1)} %get-tuple-element.11.dv_ref), custom_call_target="tpu_custom_call" | custom-call | tf_op jit(solution)/shard_map/pallas_call | solution.py:419

commit v8 on v7

--- a/solution.py
+++ b/solution.py
@@ -92,7 +92,7 @@
     def rows(off, size):
         return pl.ds(off, size)
 
-    kv_s, kx_s, re_s, le_s, xo_s = in_sem.at[0], out_sem.at[0], out_sem.at[1], out_sem.at[2], out_sem.at[3]
+    kv_s, kx_s, re_s, le_s, xo_s = in_sem.at[0], in_sem.at[3], in_sem.at[1], out_sem.at[0], in_sem.at[4]
     last = pl.ds(LOFF[-1], LSIZE[-1])
     whole = (NL, 0, ROWS)
     halves = ((0, 0, XCH), (NL - 1, XCH, XCH))
@@ -221,6 +221,8 @@
         own[0, off:off + XCH] = dk
         own[1, off:off + XCH] = dv
 
+    sib_row.wait_send()
+    sib_qd.wait_send()
     pl.when(x_ret)(lambda: kv_x().start())
 
     def fetch(n):
@@ -284,6 +286,7 @@
         dk, dv = part(queries(0), kvx, XCH, XCH, x_from * ROWS, dq_rows=everything)
         xout[0] = dk
         xout[1] = dv
+        far_qd.wait_send()
         give_x().start()
 
     pl.when(has_l & (rank != 2))(lambda: lstep(NL - 1))
@@ -343,12 +346,9 @@
     pl.when(has_r)(lambda: kv_right(*whole).wait_send())
     pl.when(chip == 3)(lambda: bounce_on().wait_send())
     pl.when(x_ret)(lambda: kv_x().wait_send())
-    sib_qd.wait_send()
-    sib_row.wait_send()
 
     @pl.when(far_left)
     def _():
-        far_qd.wait_send()
         far_row.wait_send()
         give_x().wait_send()
 
@@ -411,7 +411,7 @@
                             pltpu.VMEM((heads, rows), F32), kv, kv, pltpu.VMEM((2, 2, rows, head), BF16),
                             pltpu.VMEM((2, LSIZE[-1], head), BF16),
                             pltpu.VMEM((head, QALL), F32), sums, sums, xsum, sums, xsum, sums,
-                            dma((5,)), dma((4,)), dma((4,)), dma((NL,)), dma((2,)), dma((3,)), dma((1,)), dma((1,))],
+                            dma((5,)), dma((1,)), dma((4,)), dma((NL,)), dma((2,)), dma((3,)), dma((1,)), dma((1,))],
             compiler_params=pltpu.CompilerParams(collective_id=0, has_side_effects=True,
                                                  vmem_limit_bytes=48 << 20),
         )(*[pltpu.with_memory_space_constraint(a, pltpu.HBM) for a in (

time: 22.1 us -> 22 us (level)
  no operation moved by 1% of the time
where the time goes in v8:
time: 22 us; the launch traced here: 21.9 us
  Pallas kernels  21.1 us (96%)
  between operations  0.8 us (4%)
    pallas_call x1, Pallas kernels, local(): pl.pallas_call(kernel, out_shape=(pltpu.VMEM((QALL, head), BF16), pltpu.V...  20.3 us
    pallas_call x1, Pallas kernels, local(): pl.pallas_call(write_out, out_shape=(jax.ShapeDtypeStruct(dq.shape, BF16)...  0.86 us

profile of v8, /device:TPU:3, one launch (start us, length us, event | category | flops | bytes accessed | tf_op | source)
XLA Modules:
  0.0 21.9 jit_solution(12693677038696264293)
XLA Ops:
  0.6 20.3 %shard_map.94 = (bf16[1536,128]{1,0:T(8,128)(2,1)S(1)}, bf16[512,128]{1,0:T(8,128)(2,1)S(1)}, bf16[512,128]{1,0:T(8,128)(2,1)S(1)}) custom-call(s32[14]{0:T(128)} %cu_hbm.1, bf16[3,512,128]{2,1,0:T(8,128)(2,1)} %bitcast.7, bf16[512,128]{1,0:T(8,128)(2,1)} %k_hbm.1, bf16[512,128]{1,0:T(8,128)(2,1)} %v_hbm.1, bf16[3,512,128]{2,1,0:T(8,128)(2,1)} %bitcast.8, ...), custom_call_target="tpu_custom_call" | custom-call | tf_op jit(solution)/shard_map/pallas_call | solution.py:404
  20.9 0.9 %shard_map.95 = (bf16[1536,128]{1,0:T(8,128)(2,1)}, bf16[512,128]{1,0:T(8,128)(2,1)}, bf16[512,128]{1,0:T(8,128)(2,1)}) custom-call(bf16[1536,128]{1,0:T(8,128)(2,1)S(1)} %get-tuple-element.9.dq_ref, bf16[512,128]{1,0:T(8,128)(2,1)S(1)} %get-tuple-element.10.dk_ref, bf16[512,128]{1,0:T(8,128)(2,1)S(1)} %get-tuple-element.11.dv_ref), custom_call_target="tpu_custom_call" | custom-call | tf_op jit(solution)/shard_map/pallas_call | solution.py:419
